TPU v7x, 32 devices: a whole 2x2x4 slice. The times are simulated.
32 devices in a mesh: section: 4 (over y, x), owner: 8 (over z, core).
Axes of the slice: x: 2, y: 2, z: 4, core: 2. Of those that a mesh axis runs over, the one named last changes fastest.
Arguments:
- weights: bfloat16 [4, 1024, 1024], P('section'), may hold values from -0.1875 to 0.1875
- inputs: bfloat16 [4, 4, 2048, 1024], P('section', None, 'owner'), may hold values from -6 to 6
- preact: bfloat16 [4, 4, 2048, 1024], P('section', None, 'owner'), may hold values from -6 to 6
- cotangent: bfloat16 [4, 2048, 1024], P(None, 'owner'), may hold values from -6 to 6
- embeddings: bfloat16 [4, 2048, 32, 128], P(None, ('owner', 'section')), may hold values from -6 to 6
- row_ids: int32 [4, 2048, 32], P(None, ('owner', 'section')), may hold values from 0 to 511
Outputs:
- weight_grad: float32 [4, 1024, 1024], P('section', 'owner')
- table_grad: float32 [32, 512, 128], P('owner', 'section')
All inputs are finite; a program needn't handle non-finite values.
Results may differ from a plain program's by a relative error of at most 0.0064.
Values may be sent and summed in bfloat16 or wider, within the bound.
No kernel may reach another device: no remote copies, remote signals or barrier semaphores. Data moves between devices by JAX's collectives and lax.ppermute only.
A program may use at most 128 MiB of HBM per device.

v0:
```python
import functools
import math

import jax
import jax.numpy as jnp
from jax import lax
from jax.experimental import pallas as pl
from jax.experimental.pallas import tpu as pltpu
from jax.sharding import Mesh, PartitionSpec as P


TROWS = 512
STREAMS = 2
GROUPS = 2
NEAR_SLOTS = 4


def pair_body(where_ref, *rest, features, per_far, group_size, row_split, marks):
    piece_refs, emb_ref = rest[: len(marks)], rest[len(marks)]
    out_refs, held = rest[len(marks) + 1 : -1], rest[-1]
    flat = piece_refs[0][...]
    for mark, ref in zip(marks[1:], piece_refs[1:]):
        flat = jnp.where(where_ref[0] == mark, ref[...], flat)
    square = flat.reshape(flat.shape[0], features, features).astype(jnp.float32)
    both = (square + jnp.swapaxes(square, 1, 2)).astype(jnp.bfloat16)
    grads = lax.dot_general(
        both, emb_ref[0], (((2,), (1,)), ((0,), (0,))), preferred_element_type=jnp.float32
    ).astype(jnp.bfloat16)
    held[...] = jnp.swapaxes(grads, 0, 1)
    for turn, out_ref in enumerate(out_refs):
        for place in range(out_ref.shape[0]):
            far, rest_of = place // per_far, place % per_far
            slot = (far * group_size + where_ref[1 + turn]) * per_far + rest_of
            out_ref[place] = held[lax.div(slot, row_split)]


def pair_grads(where, pieces, marks, embeddings, group, slots, per_far, group_size, row_split):
    _, rows, features, emb_width = embeddings.shape
    samples, hidden = pieces[0].shape
    steps = samples // rows
    count = slots // group_size
    shape = jax.ShapeDtypeStruct((count, samples, emb_width), jnp.bfloat16)
    grid_spec = pltpu.PrefetchScalarGridSpec(
        num_scalar_prefetch=1,
        grid=(steps,),
        in_specs=[pl.BlockSpec((rows, hidden), lambda i, where: (i, 0))] * len(pieces)
        + [
            pl.BlockSpec(
                (1, rows, features, emb_width), lambda i, where: (group * steps + i, 0, 0, 0)
            )
        ],
        out_specs=[pl.BlockSpec((count, rows, emb_width), lambda i, where: (0, i, 0))]
        * group_size,
        scratch_shapes=[pltpu.VMEM((features, rows, emb_width), jnp.bfloat16)],
    )
    return pl.pallas_call(
        functools.partial(
            pair_body,
            features=features,
            per_far=per_far,
            group_size=group_size,
            row_split=row_split,
            marks=marks,
        ),
        grid_spec=grid_spec,
        out_shape=[shape] * group_size,
        compiler_params=pltpu.CompilerParams(vmem_limit_bytes=24 * 2**20),
        cost_estimate=pl.CostEstimate(
            flops=16 * samples * features * features * emb_width,
            bytes_accessed=samples * (features * emb_width * 4 + hidden * 8),
            transcendentals=0,
        ),
        name="pair_grads",
    )(where, *pieces, embeddings)


def row_sums_body(ids_ref, *rest, rows):
    arrived_refs, out_ref = rest[:-1], rest[-1]
    width = arrived_refs[0].shape[1]
    sources = len(arrived_refs)
    step = 2 if sources % 2 == 0 else 1
    positions = lax.broadcasted_iota(jnp.int32, (rows, step * width), 0)
    total = None
    for source in range(0, sources, step):
        places = ids_ref[0, :, source * width : (source + step) * width]
        left = jnp.where(positions == places, 1.0, 0.0).astype(jnp.bfloat16)
        right = jnp.concatenate([arrived_refs[source + i][0] for i in range(step)], axis=0)
        part = jnp.dot(left, right, preferred_element_type=jnp.float32)
        total = part if total is None else total + part
    out_ref[:, 0] = total.astype(out_ref.dtype).reshape(out_ref.shape[0], -1, total.shape[1])


def row_sums(ids, arrived, rows, parts):
    slots, width, emb = arrived[0].shape
    sources = len(arrived)
    in_specs = [pl.BlockSpec((1, 1, sources * width), lambda s: (s, 0, 0))]
    in_specs += [pl.BlockSpec((1, width, emb), lambda s: (s, 0, 0))] * sources
    return pl.pallas_call(
        functools.partial(row_sums_body, rows=rows),
        grid=(slots,),
        in_specs=in_specs,
        out_specs=pl.BlockSpec((parts, 1, rows // parts, emb), lambda s: (0, s, 0, 0)),
        out_shape=jax.ShapeDtypeStruct((parts, slots, rows // parts, emb), jnp.bfloat16),
        compiler_params=pltpu.CompilerParams(vmem_limit_bytes=16 * 2**20),
        cost_estimate=pl.CostEstimate(
            flops=2 * slots * rows * sources * width * emb,
            bytes_accessed=sources * slots * width * emb * 2 + slots * rows * emb * 2,
            transcendentals=0,
        ),
        name="row_sums",
    )(ids, *arrived)


def flip_body(in_ref, out_ref):
    block = in_ref[0, :, 0]
    out_ref[...] = block.reshape(-1, block.shape[-1]).T


def flip(layer_in):
    groups, in_group, sections, rows, hidden = layer_in.shape
    chunk_count = groups * sections
    return pl.pallas_call(
        flip_body,
        grid=(chunk_count,),
        in_specs=[
            pl.BlockSpec(
                (1, in_group, 1, rows, hidden),
                lambda c: (c // sections, 0, sections - 1 - c % sections, 0, 0),
            )
        ],
        out_specs=pl.BlockSpec((hidden, in_group * rows), lambda c: (0, c)),
        out_shape=jax.ShapeDtypeStruct(
            (hidden, chunk_count * in_group * rows), layer_in.dtype
        ),
        cost_estimate=pl.CostEstimate(
            flops=2 * layer_in.size * 256, bytes_accessed=layer_in.size * 4, transcendentals=0
        ),
        compiler_params=pltpu.CompilerParams(vmem_limit_bytes=16 * 2**20),
        name="flip",
    )(layer_in)


def weight_half_body(where_ref, flipped_ref, *rest, slots, far_slots, shifts, spots, merged):
    slope_refs = rest[:slots]
    came_ref = rest[slots] if merged else None
    out_refs, left, held, sems = rest[slots + merged : -3], rest[-3], rest[-2], rest[-1]
    section = where_ref[0]
    chunk_count = held.shape[0]
    stacks, unit, _ = left.shape
    blocks = []
    for turn in range(stacks):
        stack = spots(where_ref[2], turn)
        row = pl.multiple_of((stack * where_ref[3] + where_ref[1]) * unit, unit)
        blocks.append(
            pltpu.make_async_copy(
                flipped_ref.at[pl.ds(row, unit), :], left.at[turn], sems.at[chunk_count + turn]
            )
        )
    for copy in blocks:
        copy.start()
    for pos, shift in enumerate(shifts):

        @pl.when(section == pos)
        def _():
            copies = [
                pltpu.make_async_copy(slope_refs[chunk + shift], held.at[chunk], sems.at[chunk])
                for chunk in range(chunk_count)
                if chunk + shift < far_slots
            ]
            for copy in copies:
                copy.start()
            for chunk in range(len(copies), chunk_count):
                held[chunk] = slope_refs[chunk + shift][...]
            for copy in copies:
                copy.wait()

    for copy in blocks:
        copy.wait()
    right = held[...].reshape(left.shape[2], -1)
    total = jnp.dot(
        left[...].reshape(stacks * unit, -1), right, preferred_element_type=jnp.float32
    )
    if merged:
        parts = []
        for turn in range(stacks):
            row = pl.multiple_of(spots(where_ref[2], turn) * unit, unit)
            parts.append(came_ref[pl.ds(row, unit), :].astype(jnp.float32))
        total = total + jnp.concatenate(parts, axis=0)
    done = 0
    for out_ref in out_refs:
        rows = out_ref.shape[0]
        out_ref[...] = total[done : done + rows].astype(out_ref.dtype)
        done += rows


def weight_half(where, flipped, slopes, shifts, stacks, spots, came=None):
    hidden = slopes[0].shape[1]
    chunk_rows = slopes[0].shape[0]
    chunk_count = flipped.shape[1] // chunk_rows
    rows = flipped.shape[0] // 2
    unit = rows // stacks
    far_slots = len(slopes) - NEAR_SLOTS
    in_specs = [pl.BlockSpec(memory_space=pl.ANY)] * (1 + far_slots)
    in_specs += [pl.BlockSpec(memory_space=pltpu.VMEM)] * NEAR_SLOTS
    args = [flipped] + list(slopes)
    if came is None:
        shapes = [jax.ShapeDtypeStruct((rows, hidden), jnp.bfloat16)]
    else:
        in_specs.append(pl.BlockSpec(came.shape, lambda i, where: (0, 0)))
        args.append(came)
        shapes = [
            jax.ShapeDtypeStruct((unit, hidden), jnp.float32),
            jax.ShapeDtypeStruct((unit, hidden), jnp.float32),
            jax.ShapeDtypeStruct((2 * unit, hidden), jnp.bfloat16),
        ]
    grid_spec = pltpu.PrefetchScalarGridSpec(
        num_scalar_prefetch=1,
        grid=(1,),
        in_specs=in_specs,
        out_specs=[pl.BlockSpec(shape.shape, lambda i, where: (0, 0)) for shape in shapes],
        scratch_shapes=[
            pltpu.VMEM((stacks, unit, flipped.shape[1]), jnp.bfloat16),
            pltpu.VMEM((chunk_count, chunk_rows, hidden), jnp.bfloat16),
            pltpu.SemaphoreType.DMA((chunk_count + stacks,)),
        ],
    )
    return pl.pallas_call(
        functools.partial(
            weight_half_body,
            slots=len(slopes),
            far_slots=far_slots,
            shifts=shifts,
            spots=spots,
            merged=came is not None,
        ),
        grid_spec=grid_spec,
        out_shape=shapes,
        compiler_params=pltpu.CompilerParams(vmem_limit_bytes=24 * 2**20),
        cost_estimate=pl.CostEstimate(
            flops=flipped.size * hidden, bytes_accessed=flipped.size * 6, transcendentals=0
        ),
        name="weight_half",
    )(where, *args)


def natural(stack, turn):
    return turn


def from_own(stack, turn):
    return ((stack // 2) ^ (turn % 2)) * 2 + ((stack % 2) ^ (turn // 2))


def exchange(blocks, axis):
    size = lax.axis_size(axis)
    place = lax.axis_index(axis)
    if size > 8:
        came = lax.all_to_all(
            blocks.astype(jnp.bfloat16), axis, split_axis=0, concat_axis=0, tiled=True
        )
        return jnp.sum(came.astype(jnp.float32), axis=0)
    total = lax.dynamic_index_in_dim(blocks, place, 0, False).astype(jnp.float32)
    for shift in range(1, size):
        sent = lax.dynamic_index_in_dim(blocks, (place + shift) % size, 0, False)
        turn = [(i, (i + shift) % size) for i in range(size)]
        came = lax.ppermute(sent.astype(jnp.bfloat16), axis, turn)
        total = total + came.astype(jnp.float32)
    return total


def after(value, *others):
    return lax.optimization_barrier((value,) + others)[0]


def per_device(weights, inputs, preact, cotangent, embeddings, row_ids):
    sections = lax.axis_size("section")
    fars = lax.axis_size("far")
    nears = lax.axis_size("near")
    stacks = fars * nears
    cores = lax.axis_size("core")
    owners = stacks * cores
    section_pos = lax.axis_index("section")
    core_pos = lax.axis_index("core")
    stack_pos = lax.axis_index("far") * nears + lax.axis_index("near")
    micro_count, batch_rows, hidden = cotangent.shape
    features = embeddings.shape[2]
    emb_width = embeddings.shape[3]
    quarter = batch_rows // sections
    row_split = max(1, owners // features)
    slot_count = features * row_split // owners
    grad_scale = 1.0 / math.sqrt(micro_count * batch_rows * owners)
    last = sections - 1
    is_last = section_pos == last
    layer_w = weights[0]

    in_group = micro_count // GROUPS
    order = list(range(last, -1, -1))
    chunk_count = GROUPS * sections
    chunk_rows = in_group * quarter
    view = (GROUPS, in_group, sections, quarter, hidden)
    cot_view = cotangent.reshape(view)
    pre_view = preact[0].reshape(view)

    down = [(i, i - 1) for i in range(1, sections)]
    fill = STREAMS * last
    total_slots = chunk_count + fill
    shifts = [STREAMS * (last - pos) for pos in range(sections)]
    shift_now = STREAMS * (last - section_pos)
    unit = hidden // owners
    in_view = inputs[0].reshape(view)
    flipped = None
    group_size = nears * cores
    near_core = lax.axis_index("near") * cores + core_pos
    held_slots = (
        jnp.arange(fars, dtype=jnp.int32)[:, None] * (group_size * slot_count)
        + near_core * slot_count
        + jnp.arange(slot_count, dtype=jnp.int32)[None, :]
    ).reshape(fars * slot_count)

    partners = [near_core]
    ways = [None]
    for turn in range(1, group_size):
        flip_near, flip_core = turn // cores, turn % cores
        near, core = near_core // cores, near_core % cores
        partners.append((near ^ flip_near) * cores + (core ^ flip_core))
        ways.append(
            [
                (i, (i // cores ^ flip_near) * cores + (i % cores ^ flip_core))
                for i in range(group_size)
            ]
        )

    def to_holders(blocks):
        came = [blocks[0]]
        for turn in range(1, group_size):
            came.append(lax.ppermute(blocks[turn], ("near", "core"), ways[turn]))
        return came

    received = {}
    slopes = []
    pieces = {}
    waiting = []
    arrived = []
    ids = None
    for slot in range(total_slots):
        spot = jnp.clip(slot - shift_now, 0, chunk_count - 1)
        zero = jnp.zeros_like(spot)
        if slot >= 2 * STREAMS and slot % STREAMS == 0:
            pre_view = after(pre_view, passed)
        pre_now = lax.dynamic_slice(
            pre_view,
            (lax.div(spot, sections), zero, last - lax.rem(spot, sections), zero, zero),
            (1, in_group, 1, quarter, hidden),
        ).reshape(chunk_rows, hidden)
        if slot < chunk_count:
            incoming = cot_view[slot // sections, :, order[slot % sections]]
            incoming = incoming.reshape(chunk_rows, hidden)
            if slot >= STREAMS:
                incoming = jnp.where(is_last, incoming, received.pop(slot - STREAMS))
        else:
            incoming = received.pop(slot - STREAMS)
        slope = jnp.where(pre_now > 0, incoming, jnp.zeros_like(incoming))
        slopes.append(slope)
        passed = lax.dot_general(
            slope, layer_w, (((1,), (1,)), ((), ())), preferred_element_type=jnp.float32
        ).astype(jnp.bfloat16)
        chunk = slot - fill
        target = order[chunk % sections] if chunk >= 0 else None
        in_chain = slot < total_slots - STREAMS
        if in_chain:
            pairs = down + [(0, last)] if target == last else down
            received[slot] = lax.ppermute(passed, "section", pairs)
        if chunk >= 0:
            if target == last and in_chain:
                pieces[chunk] = received[slot]
            elif target == 0:
                pieces[chunk] = passed
            else:
                waiting.append((chunk, target, slot, passed))
        if in_chain and slot % STREAMS != STREAMS - 1:
            continue
        if ids is None and slot > STREAMS:
            ids = jnp.transpose(after(row_ids, passed), (2, 0, 1))
            ids = jnp.repeat(ids.reshape(features, micro_count * quarter), row_split, axis=0)
            ids = ids.reshape(fars, group_size, slot_count, micro_count * quarter)
            ids = [
                lax.dynamic_index_in_dim(ids, partner, 1, False).reshape(
                    fars * slot_count, micro_count * quarter
                )
                for partner in partners
            ]
            ids = to_holders(ids)
            ids = jnp.concatenate(
                [
                    source[:, group * chunk_rows : (group + 1) * chunk_rows]
                    for group in range(GROUPS)
                    for source in ids
                ],
                axis=1,
            )
            if row_split > 1:
                ids = ids - ((held_slots % row_split) * TROWS)[:, None]
            ids = ids[:, None, :]
        elif ids is not None and flipped is None and unit % 128 == 0 and fars == nears == cores == 2:
            flipped = flip(after(in_view, passed))
        ready = None
        if chunk >= 0:
            group = chunk // sections - (0 if chunk % sections == last else 1)
            if group >= 0 and all(group * sections + q in pieces for q in range(sections)):
                ready = group
        for sent, target, sent_slot, held in waiting:
            pieces[sent] = lax.ppermute(after(held, passed), "section", [(0, target)])
        waiting = []
        final = chunk == chunk_count - 1
        if final:
            ready = GROUPS - 1
        if ready is None:
            continue
        ready_pieces = [pieces.pop(ready * sections + q) for q in range(sections)]
        where = jnp.stack([section_pos] + partners).astype(jnp.int32)
        blocks = pair_grads(
            where,
            ready_pieces,
            order,
            embeddings,
            ready,
            features * row_split,
            slot_count,
            group_size,
            row_split,
        )
        arrived.append(to_holders(blocks))

    if flipped is not None:
        where = jnp.stack(
            [section_pos, 1 - core_pos, stack_pos, jnp.full_like(section_pos, cores)]
        ).astype(jnp.int32)
        (side,) = weight_half(where, flipped, slopes, shifts, stacks, natural)
        came = lax.ppermute(side, "core", [(0, 1), (1, 0)])
        where = jnp.stack(
            [section_pos, core_pos, stack_pos, jnp.full_like(section_pos, cores)]
        ).astype(jnp.int32)
        own_rows, far_rows, near_rows = weight_half(
            where, flipped, slopes, shifts, stacks, from_own, came
        )
        near_came = lax.ppermute(near_rows, "near", [(0, 1), (1, 0)]).astype(jnp.float32)
    table = row_sums(ids, [block for group in arrived for block in group], TROWS, sections)

    if flipped is not None:
        far_sum = (far_rows + near_came[unit:]).astype(jnp.bfloat16)
        far_came = lax.ppermute(far_sum, "far", [(0, 1), (1, 0)]).astype(jnp.float32)
        weight_grad = (own_rows + near_came[:unit] + far_came) * grad_scale
    else:
        line = jnp.concatenate(slopes, 0)
        flat_slope = lax.dynamic_slice_in_dim(
            line,
            STREAMS * (last - section_pos) * chunk_rows,
            micro_count * batch_rows,
            0,
        )
        in_order = in_view[:, :, jnp.asarray(order)]
        in_order = jnp.swapaxes(in_order, 1, 2).reshape(micro_count * batch_rows, hidden)
        full = lax.dot_general(
            in_order, flat_slope, (((0,), (0,)), ((), ())), preferred_element_type=jnp.float32
        ).reshape(stacks, cores, unit, hidden)
        summed = lax.dynamic_index_in_dim(full, core_pos, 1, False)
        for shift in range(1, cores):
            side = lax.dynamic_index_in_dim(full, (core_pos + shift) % cores, 1, False)
            turn = [(i, (i + shift) % cores) for i in range(cores)]
            came = lax.ppermute(side.astype(jnp.bfloat16), "core", turn)
            summed = summed + came.astype(jnp.float32)
        weight_grad = exchange(summed, ("far", "near")) * grad_scale

    table = exchange(table, "section")
    table = table.reshape(fars, slot_count, TROWS // sections, emb_width)
    table_grad = exchange(table, "far")
    table_grad = table_grad * grad_scale
    return (weight_grad[None], table_grad)


def solution(mesh):
    sections, owners = mesh.devices.shape
    cores = 2 if owners % 2 == 0 else 1
    stacks = owners // cores
    nears = 2 if stacks % 2 == 0 else 1
    inner = Mesh(
        mesh.devices.reshape(sections, stacks // nears, nears, cores),
        ("section", "far", "near", "core"),
    )
    own = ("far", "near", "core")

    return jax.shard_map(
        per_device,
        mesh=inner,
        in_specs=(
            P("section", None, None),
            P("section", None, own, None),
            P("section", None, own, None),
            P(None, own, None),
            P(None, own + ("section",), None, None),
            P(None, own + ("section",), None),
        ),
        out_specs=(P("section", own, None), P(own, "section", None)),
        check_vma=False,
    )
```

profile of v0, /device:TPU:0, one launch (start us, length us, event | category | flops | bytes accessed | tf_op | source)
XLA Modules:
  0.0 179.7 jit_solution(14449560379257834062)
XLA Ops:
  9.7 2.3 %fusion.78 = (bf16[1,2,1,64,1024]{4,3,2,1,0:T(8,128)(2,1)S(1)}, bf16[1,2,1,64,1024]{4,3,2,1,0:T(8,128)(2,1)S(1)}, bf16[1,2,1,64,1024]{4,3,2,1,0:T(8,128)(2,1)}, ...) fusion(bf16[2,2,4,64,1024]{4,3,2,1,0:T(8,128)(2,1)} %bitcast.194), kind=kLoop, calls=%fused_computation.106 | loop fusion | bytes 3145728 | tf_op jit(solution)/shard_map/slice | solution.py:356
  12.0 9.1 %collective-permute-done = bf16[128,1024]{1,0:T(8,128)(2,1)S(1)} collective-permute-done((bf16[128,1024]{1,0:T(8,128)(2,1)}, bf16[128,1024]{1,0:T(8,128)(2,1)S(1)}, u32[]{:S(2)}, u32[]{:S(2)}) %collective-permute-start) | collective-permute-done | bytes 262176 | tf_op jit(solution)/shard_map/ppermute | solution.py:372
  39.4 10.2 %collective-permute-done.3 = bf16[128,1024]{1,0:T(8,128)(2,1)S(1)} collective-permute-done((bf16[128,1024]{1,0:T(8,128)(2,1)S(1)}, bf16[128,1024]{1,0:T(8,128)(2,1)S(1)}, u32[]{:S(2)}, u32[]{:S(2)}) %collective-permute-start.3) | collective-permute-done | bytes 262176 | tf_op jit(solution)/shard_map/ppermute | solution.py:372
  57.1 10.1 %collective-permute-done.5 = bf16[128,1024]{1,0:T(8,128)(2,1)S(1)} collective-permute-done((bf16[128,1024]{1,0:T(8,128)(2,1)S(1)}, bf16[128,1024]{1,0:T(8,128)(2,1)S(1)}, u32[]{:S(2)}, u32[]{:S(2)}) %collective-permute-start.5) | collective-permute-done | bytes 262176 | tf_op jit(solution)/shard_map/ppermute | solution.py:372
  70.4 3.9 %collective-permute-start.6 = (bf16[128,1024]{1,0:T(8,128)(2,1)S(1)}, bf16[128,1024]{1,0:T(8,128)(2,1)S(1)}, u32[]{:S(2)}, u32[]{:S(2)}) collective-permute-start(bf16[128,1024]{1,0:T(8,128)(2,1)S(1)} %fusion.49), channel_id=1, source_target_pairs={{8,0},{16,8},{24,16},{0,24},{9,1},{17,9},{25,17},{1,25},{10,2},{18... | collective-permute-start | bytes 786440 | tf_op jit(solution)/shard_map/ppermute | solution.py:372
  74.3 2.8 %collective-permute-start.18 = (bf16[128,1024]{1,0:T(8,128)(2,1)S(1)}, bf16[128,1024]{1,0:T(8,128)(2,1)S(1)}, u32[]{:S(2)}, u32[]{:S(2)}) collective-permute-start(bf16[128,1024]{1,0:T(8,128)(2,1)S(1)} %fusion.46), channel_id=1, source_target_pairs={{0,16},{1,17},{2,18},{3,19},{4,20},{5,21},{6,22},{7,23}} | collective-permute-start | bytes 786440 | tf_op jit(solution)/shard_map/ppermute | solution.py:412
  77.3 2.6 %collective-permute-done.7 = bf16[128,1024]{1,0:T(8,128)(2,1)S(1)} collective-permute-done((bf16[128,1024]{1,0:T(8,128)(2,1)S(1)}, bf16[128,1024]{1,0:T(8,128)(2,1)S(1)}, u32[]{:S(2)}, u32[]{:S(2)}) %collective-permute-start.7) | collective-permute-done | bytes 262176 | tf_op jit(solution)/shard_map/ppermute | solution.py:372
  82.0 3.0 %collective-permute-done.6.rest_0_ = bf16[128,1024]{1,0:T(8,128)(2,1)S(1)} collective-permute-done((bf16[128,1024]{1,0:T(8,128)(2,1)S(1)}, bf16[128,1024]{1,0:T(8,128)(2,1)S(1)}, u32[]{:S(2)}, u32[]{:S(2)}) %collective-permute-start.6) | collective-permute-done | bytes 262176 | tf_op jit(solution)/shard_map/ppermute | solution.py:372
  87.2 5.2 %collective-permute-start.19 = (bf16[128,1024]{1,0:T(8,128)(2,1)S(1)}, bf16[128,1024]{1,0:T(8,128)(2,1)S(1)}, u32[]{:S(2)}, u32[]{:S(2)}) collective-permute-start(bf16[128,1024]{1,0:T(8,128)(2,1)S(1)} %fusion.55), channel_id=1, source_target_pairs={{0,8},{1,9},{2,10},{3,11},{4,12},{5,13},{6,14},{7,15}} | collective-permute-start | bytes 786440 | tf_op jit(solution)/shard_map/ppermute | solution.py:412
  98.6 2.0 %pair_grads.2 = (bf16[8,128,128]{2,1,0:T(8,128)(2,1)S(1)}, bf16[8,128,128]{2,1,0:T(8,128)(2,1)S(1)}, bf16[8,128,128]{2,1,0:T(8,128)(2,1)S(1)}, bf16[8,128,128]{2,1,0:T(8,128)(2,1)S(1)}) custom-call(s32[5]{0:T(128)S(1)} %stack.52.where_ref, bf16[128,1024]{1,0:T(8,128)(2,1)S(1)} %collective-permute-done.6.rest_0_, ...), custom_call_target="tpu_custom_call" | custom-call | flops 268435456 | bytes 3145728 | tf_op jit(solution)/shard_map/pair_grads/pallas_call | solution.py:56
  102.3 6.7 %collective-permute-start.23 = (bf16[128,1024]{1,0:T(8,128)(2,1)S(1)}, bf16[128,1024]{1,0:T(8,128)(2,1)S(1)}, u32[]{:S(2)}, u32[]{:S(2)}) collective-permute-start(bf16[128,1024]{1,0:T(8,128)(2,1)S(1)} %fusion.58), channel_id=1, source_target_pairs={{0,16},{1,17},{2,18},{3,19},{4,20},{5,21},{6,22},{7,23}} | collective-permute-start | bytes 786440 | tf_op jit(solution)/shard_map/ppermute | solution.py:412
  110.0 2.4 %collective-permute-start.24 = (bf16[128,1024]{1,0:T(8,128)(2,1)S(1)}, bf16[128,1024]{1,0:T(8,128)(2,1)S(1)}, u32[]{:S(2)}, u32[]{:S(2)}) collective-permute-start(bf16[128,1024]{1,0:T(8,128)(2,1)S(1)} %fusion.64), channel_id=1, source_target_pairs={{0,8},{1,9},{2,10},{3,11},{4,12},{5,13},{6,14},{7,15}} | collective-permute-start | bytes 786440 | tf_op jit(solution)/shard_map/ppermute | solution.py:412
  112.5 2.2 %weight_half.2 = bf16[512,1024]{1,0:T(8,128)(2,1)S(1)} custom-call(s32[4]{0:T(128)S(1)} %pad_add_fusion.where_ref, bf16[1024,1024]{1,0:T(8,128)(2,1)S(1)} %flip.1.flipped_ref, bf16[128,1024]{1,0:T(8,128)(2,1)S(1)} %bitcast.180, bf16[128,1024]{1,0:T(8,128)(2,1)S(1)} %bitcast.183, bf16[128,1024]{1,0:T(8,128)(2,1)S(1)} %bitcast_select_fusion.9.rest_2_, ...), custom_call_target="tpu_custom_call" | custom-call | flops 1073741824 | bytes 6291456 | tf_op jit(solution)/shard_map/weight_half/pallas_call | solution.py:227
  121.3 2.7 %collective-permute-done.22.rest_3_ = bf16[8,128,128]{2,1,0:T(8,128)(2,1)S(1)} collective-permute-done((bf16[8,128,128]{2,1,0:T(8,128)(2,1)S(1)}, bf16[8,128,128]{2,1,0:T(8,128)(2,1)S(1)}, u32[]{:S(2)}, u32[]{:S(2)}) %collective-permute-start.22) | collective-permute-done | bytes 262176 | tf_op jit(solution)/shard_map/ppermute | solution.py:336
  124.1 6.5 %collective-permute-done.26.rest_6_ = bf16[8,128,128]{2,1,0:T(8,128)(2,1)S(1)} collective-permute-done((bf16[8,128,128]{2,1,0:T(8,128)(2,1)S(1)}, bf16[8,128,128]{2,1,0:T(8,128)(2,1)S(1)}, u32[]{:S(2)}, u32[]{:S(2)}) %collective-permute-start.26) | collective-permute-done | bytes 262176 | tf_op jit(solution)/shard_map/ppermute | solution.py:336
  130.6 4.3 %collective-permute-done.27.rest_7_ = bf16[8,128,128]{2,1,0:T(8,128)(2,1)S(1)} collective-permute-done((bf16[8,128,128]{2,1,0:T(8,128)(2,1)S(1)}, bf16[8,128,128]{2,1,0:T(8,128)(2,1)S(1)}, u32[]{:S(2)}, u32[]{:S(2)}) %collective-permute-start.27) | collective-permute-done | bytes 262176 | tf_op jit(solution)/shard_map/ppermute | solution.py:336
  134.9 3.7 %row_sums.1 = bf16[4,8,128,128]{3,2,1,0:T(8,128)(2,1)S(1)} custom-call(s32[8,1,1024]{2,1,0:T(1,128)S(1)} %broadcast_in_dim.7.ids_ref, bf16[8,128,128]{2,1,0:T(8,128)(2,1)S(1)} %get-tuple-element.35.rest_0_, bf16[8,128,128]{2,1,0:T(8,128)(2,1)S(1)} %collective-permute-done.20.rest_1_, bf16[8,128,128]{2,1,0:T(8,128)(2,1)S(1)} %collective-permute-done.21.rest_2_, ...), custom_call_target="tpu_custom_call" | custom-call | flops 1073741824 | bytes 3145728 | tf_op jit(solution)/shard_map/row_sums/pallas_call | solution.py:98
  141.2 2.2 %collective-permute-start.30 = (bf16[8,128,128]{2,1,0:T(8,128)(2,1)}, bf16[8,128,128]{2,1,0:T(8,128)(2,1)}, u32[]{:S(2)}, u32[]{:S(2)}) collective-permute-start(bf16[8,128,128]{2,1,0:T(8,128)(2,1)} %get-tuple-element.65), channel_id=1, source_target_pairs={{0,24},{8,0},{16,8},{24,16},{1,25},{9,1},{17,9},{25,17},{2,26},{10... | collective-permute-start | bytes 786440 | tf_op jit(solution)/shard_map/ppermute | solution.py:266
  145.0 3.0 %weight_half.3 = (f32[128,1024]{1,0:T(8,128)S(1)}, f32[128,1024]{1,0:T(8,128)S(1)}, bf16[256,1024]{1,0:T(8,128)(2,1)}) custom-call(s32[4]{0:T(128)S(1)} %pad_add_fusion.1.where_ref, bf16[1024,1024]{1,0:T(8,128)(2,1)S(1)} %flip.1.flipped_ref, bf16[128,1024]{1,0:T(8,128)(2,1)S(1)} %bitcast.181, bf16[128,1024]{1,0:T(8,128)(2,1)S(1)} %bitcast.184, ...), custom_call_target="tpu_custom_call" | custom-call | flops 1073741824 | bytes 6291456 | tf_op jit(solution)/shard_map/weight_half/pallas_call | solution.py:227
  150.9 4.3 %collective-permute-done.30 = bf16[8,128,128]{2,1,0:T(8,128)(2,1)} collective-permute-done((bf16[8,128,128]{2,1,0:T(8,128)(2,1)}, bf16[8,128,128]{2,1,0:T(8,128)(2,1)}, u32[]{:S(2)}, u32[]{:S(2)}) %collective-permute-start.30) | collective-permute-done | bytes 262176 | tf_op jit(solution)/shard_map/ppermute | solution.py:266
  157.3 2.6 %collective-permute-start.31 = (bf16[4,128,128]{2,1,0:T(8,128)(2,1)S(1)}, bf16[4,128,128]{2,1,0:T(8,128)(2,1)}, u32[]{:S(2)}, u32[]{:S(2)}) collective-permute-start(bf16[4,128,128]{2,1,0:T(8,128)(2,1)S(1)} %fusion.77), channel_id=1, source_target_pairs={{0,4},{4,0},{1,5},{5,1},{2,6},{6,2},{3,7},{7,3},{8,12},{12,8},{9,1... | collective-permute-start | bytes 393224 | tf_op jit(solution)/shard_map/ppermute | solution.py:266
  160.0 3.3 %collective-permute-done.13 = bf16[256,1024]{1,0:T(8,128)(2,1)} collective-permute-done((bf16[256,1024]{1,0:T(8,128)(2,1)}, bf16[256,1024]{1,0:T(8,128)(2,1)}, u32[]{:S(2)}, u32[]{:S(2)}) %collective-permute-start.13) | collective-permute-done | bytes 524320 | tf_op jit(solution)/shard_map/ppermute | solution.py:446
  165.5 2.4 %collective-permute-start.14 = (bf16[128,1024]{1,0:T(8,128)(2,1)}, bf16[128,1024]{1,0:T(8,128)(2,1)S(1)}, u32[]{:S(2)}, u32[]{:S(2)}) collective-permute-start(bf16[128,1024]{1,0:T(8,128)(2,1)} %fusion.70), channel_id=1, source_target_pairs={{0,4},{4,0},{1,5},{5,1},{2,6},{6,2},{3,7},{7,3},{8,12},{12,8},{9,1... | collective-permute-start | bytes 786440 | tf_op jit(solution)/shard_map/ppermute | solution.py:451
  169.7 8.1 %collective-permute-done.14 = bf16[128,1024]{1,0:T(8,128)(2,1)S(1)} collective-permute-done((bf16[128,1024]{1,0:T(8,128)(2,1)}, bf16[128,1024]{1,0:T(8,128)(2,1)S(1)}, u32[]{:S(2)}, u32[]{:S(2)}) %collective-permute-start.14) | collective-permute-done | bytes 262176 | tf_op jit(solution)/shard_map/ppermute | solution.py:451
  (134 shorter events, 72.7 us)
Async XLA Ops:
  4.1 31.6 %collective-permute-start.2 = (bf16[128,1024]{1,0:T(8,128)(2,1)}, bf16[128,1024]{1,0:T(8,128)(2,1)}, u32[]{:S(2)}, u32[]{:S(2)}) collective-permute-start(bf16[128,1024]{1,0:T(8,128)(2,1)} %fusion.37), channel_id=1, source_target_pairs={{8,0},{16,8},{24,16},{9,1},{17,9},{25,17},{10,2},{18,10},{26,18},{... | collective-permute-start | bytes 786440 | tf_op jit(solution)/shard_map/ppermute | solution.py:372
  6.9 14.2 %collective-permute-start = (bf16[128,1024]{1,0:T(8,128)(2,1)}, bf16[128,1024]{1,0:T(8,128)(2,1)S(1)}, u32[]{:S(2)}, u32[]{:S(2)}) collective-permute-start(bf16[128,1024]{1,0:T(8,128)(2,1)} %fusion.28), channel_id=1, source_target_pairs={{8,0},{16,8},{24,16},{9,1},{17,9},{25,17},{10,2},{18,10},{26,18},{... | collective-permute-start | bytes 786440 | tf_op jit(solution)/shard_map/ppermute | solution.py:372
  24.3 27.6 %collective-permute-start.1 = (bf16[128,1024]{1,0:T(8,128)(2,1)}, bf16[128,1024]{1,0:T(8,128)(2,1)}, u32[]{:S(2)}, u32[]{:S(2)}) collective-permute-start(bf16[128,1024]{1,0:T(8,128)(2,1)} %fusion.31), channel_id=1, source_target_pairs={{8,0},{16,8},{24,16},{9,1},{17,9},{25,17},{10,2},{18,10},{26,18},{... | collective-permute-start | bytes 786440 | tf_op jit(solution)/shard_map/ppermute | solution.py:372
  37.6 12.0 %collective-permute-start.3 = (bf16[128,1024]{1,0:T(8,128)(2,1)S(1)}, bf16[128,1024]{1,0:T(8,128)(2,1)S(1)}, u32[]{:S(2)}, u32[]{:S(2)}) collective-permute-start(bf16[128,1024]{1,0:T(8,128)(2,1)S(1)} %fusion.40), channel_id=1, source_target_pairs={{8,0},{16,8},{24,16},{9,1},{17,9},{25,17},{10,2},{18,10},{26,18},{... | collective-permute-start | bytes 786440 | tf_op jit(solution)/shard_map/ppermute | solution.py:372
  50.5 18.9 %collective-permute-start.4 = (bf16[128,1024]{1,0:T(8,128)(2,1)S(1)}, bf16[128,1024]{1,0:T(8,128)(2,1)S(1)}, u32[]{:S(2)}, u32[]{:S(2)}) collective-permute-start(bf16[128,1024]{1,0:T(8,128)(2,1)S(1)} %fusion.43), channel_id=1, source_target_pairs={{8,0},{16,8},{24,16},{9,1},{17,9},{25,17},{10,2},{18,10},{26,18},{... | collective-permute-start | bytes 786440 | tf_op jit(solution)/shard_map/ppermute | solution.py:372
  53.8 13.4 %collective-permute-start.5 = (bf16[128,1024]{1,0:T(8,128)(2,1)S(1)}, bf16[128,1024]{1,0:T(8,128)(2,1)S(1)}, u32[]{:S(2)}, u32[]{:S(2)}) collective-permute-start(bf16[128,1024]{1,0:T(8,128)(2,1)S(1)} %fusion.34), channel_id=1, source_target_pairs={{8,0},{16,8},{24,16},{9,1},{17,9},{25,17},{10,2},{18,10},{26,18},{... | collective-permute-start | bytes 786440 | tf_op jit(solution)/shard_map/ppermute | solution.py:372
  68.2 11.7 %collective-permute-start.7 = (bf16[128,1024]{1,0:T(8,128)(2,1)S(1)}, bf16[128,1024]{1,0:T(8,128)(2,1)S(1)}, u32[]{:S(2)}, u32[]{:S(2)}) collective-permute-start(bf16[128,1024]{1,0:T(8,128)(2,1)S(1)} %fusion.46), channel_id=1, source_target_pairs={{8,0},{16,8},{24,16},{9,1},{17,9},{25,17},{10,2},{18,10},{26,18},{... | collective-permute-start | bytes 786440 | tf_op jit(solution)/shard_map/ppermute | solution.py:372
  70.4 14.6 %collective-permute-start.6 = (bf16[128,1024]{1,0:T(8,128)(2,1)S(1)}, bf16[128,1024]{1,0:T(8,128)(2,1)S(1)}, u32[]{:S(2)}, u32[]{:S(2)}) collective-permute-start(bf16[128,1024]{1,0:T(8,128)(2,1)S(1)} %fusion.49), channel_id=1, source_target_pairs={{8,0},{16,8},{24,16},{0,24},{9,1},{17,9},{25,17},{1,25},{10,2},{18... | collective-permute-start | bytes 786440 | tf_op jit(solution)/shard_map/ppermute | solution.py:372
  74.3 24.3 %collective-permute-start.18 = (bf16[128,1024]{1,0:T(8,128)(2,1)S(1)}, bf16[128,1024]{1,0:T(8,128)(2,1)S(1)}, u32[]{:S(2)}, u32[]{:S(2)}) collective-permute-start(bf16[128,1024]{1,0:T(8,128)(2,1)S(1)} %fusion.46), channel_id=1, source_target_pairs={{0,16},{1,17},{2,18},{3,19},{4,20},{5,21},{6,22},{7,23}} | collective-permute-start | bytes 786440 | tf_op jit(solution)/shard_map/ppermute | solution.py:412
  80.7 11.8 %collective-permute-start.9 = (bf16[128,1024]{1,0:T(8,128)(2,1)S(1)}, bf16[128,1024]{1,0:T(8,128)(2,1)S(1)}, u32[]{:S(2)}, u32[]{:S(2)}) collective-permute-start(bf16[128,1024]{1,0:T(8,128)(2,1)S(1)} %fusion.52.rest_3_), channel_id=1, source_target_pairs={{8,0},{16,8},{24,16},{9,1},{17,9},{25,17},{10,2},{18,10},{26,18},{... | collective-permute-start | bytes 786440 | tf_op jit(solution)/shard_map/ppermute | solution.py:372
  85.9 10.7 %collective-permute-start.8 = (bf16[128,1024]{1,0:T(8,128)(2,1)S(1)}, bf16[128,1024]{1,0:T(8,128)(2,1)S(1)}, u32[]{:S(2)}, u32[]{:S(2)}) collective-permute-start(bf16[128,1024]{1,0:T(8,128)(2,1)S(1)} %fusion.55), channel_id=1, source_target_pairs={{8,0},{16,8},{24,16},{9,1},{17,9},{25,17},{10,2},{18,10},{26,18},{... | collective-permute-start | bytes 786440 | tf_op jit(solution)/shard_map/ppermute | solution.py:372
  87.2 11.4 %collective-permute-start.19 = (bf16[128,1024]{1,0:T(8,128)(2,1)S(1)}, bf16[128,1024]{1,0:T(8,128)(2,1)S(1)}, u32[]{:S(2)}, u32[]{:S(2)}) collective-permute-start(bf16[128,1024]{1,0:T(8,128)(2,1)S(1)} %fusion.55), channel_id=1, source_target_pairs={{0,8},{1,9},{2,10},{3,11},{4,12},{5,13},{6,14},{7,15}} | collective-permute-start | bytes 786440 | tf_op jit(solution)/shard_map/ppermute | solution.py:412
  93.5 19.0 %collective-permute-start.11 = (bf16[128,1024]{1,0:T(8,128)(2,1)S(1)}, bf16[128,1024]{1,0:T(8,128)(2,1)S(1)}, u32[]{:S(2)}, u32[]{:S(2)}) collective-permute-start(bf16[128,1024]{1,0:T(8,128)(2,1)S(1)} %fusion.58), channel_id=1, source_target_pairs={{8,0},{16,8},{24,16},{9,1},{17,9},{25,17},{10,2},{18,10},{26,18},{... | collective-permute-start | bytes 786440 | tf_op jit(solution)/shard_map/ppermute | solution.py:372
  97.5 11.7 %collective-permute-start.10 = (bf16[128,1024]{1,0:T(8,128)(2,1)S(1)}, bf16[128,1024]{1,0:T(8,128)(2,1)S(1)}, u32[]{:S(2)}, u32[]{:S(2)}) collective-permute-start(bf16[128,1024]{1,0:T(8,128)(2,1)S(1)} %fusion.61), channel_id=1, source_target_pairs={{8,0},{16,8},{24,16},{0,24},{9,1},{17,9},{25,17},{1,25},{10,2},{18... | collective-permute-start | bytes 786440 | tf_op jit(solution)/shard_map/ppermute | solution.py:372
  100.6 18.9 %collective-permute-start.20 = (bf16[8,128,128]{2,1,0:T(8,128)(2,1)S(1)}, bf16[8,128,128]{2,1,0:T(8,128)(2,1)S(1)}, u32[]{:S(2)}, u32[]{:S(2)}) collective-permute-start(bf16[8,128,128]{2,1,0:T(8,128)(2,1)S(1)} %get-tuple-element.36), channel_id=1, source_target_pairs={{0,1},{1,0},{2,3},{3,2},{4,5},{5,4},{6,7},{7,6},{8,9},{9,8},{10,11... | collective-permute-start | bytes 786440 | tf_op jit(solution)/shard_map/ppermute | solution.py:336
  100.7 19.4 %collective-permute-start.21 = (bf16[8,128,128]{2,1,0:T(8,128)(2,1)S(1)}, bf16[8,128,128]{2,1,0:T(8,128)(2,1)S(1)}, u32[]{:S(2)}, u32[]{:S(2)}) collective-permute-start(bf16[8,128,128]{2,1,0:T(8,128)(2,1)S(1)} %get-tuple-element.37), channel_id=1, source_target_pairs={{0,2},{1,3},{2,0},{3,1},{4,6},{5,7},{6,4},{7,5},{8,10},{9,11},{10,... | collective-permute-start | bytes 786440 | tf_op jit(solution)/shard_map/ppermute | solution.py:336
  102.3 13.3 %collective-permute-start.23 = (bf16[128,1024]{1,0:T(8,128)(2,1)S(1)}, bf16[128,1024]{1,0:T(8,128)(2,1)S(1)}, u32[]{:S(2)}, u32[]{:S(2)}) collective-permute-start(bf16[128,1024]{1,0:T(8,128)(2,1)S(1)} %fusion.58), channel_id=1, source_target_pairs={{0,16},{1,17},{2,18},{3,19},{4,20},{5,21},{6,22},{7,23}} | collective-permute-start | bytes 786440 | tf_op jit(solution)/shard_map/ppermute | solution.py:412
  114.7 30.3 %collective-permute-start.12 = (bf16[512,1024]{1,0:T(8,128)(2,1)S(1)}, bf16[512,1024]{1,0:T(8,128)(2,1)S(1)}, u32[]{:S(2)}, u32[]{:S(2)}) collective-permute-start(bf16[512,1024]{1,0:T(8,128)(2,1)S(1)} %weight_half.2), channel_id=1, source_target_pairs={{0,1},{1,0},{2,3},{3,2},{4,5},{5,4},{6,7},{7,6},{8,9},{9,8},{10,11... | collective-permute-start | bytes 3145736 | tf_op jit(solution)/shard_map/ppermute | solution.py:439
  119.5 11.1 %collective-permute-start.26 = (bf16[8,128,128]{2,1,0:T(8,128)(2,1)S(1)}, bf16[8,128,128]{2,1,0:T(8,128)(2,1)S(1)}, u32[]{:S(2)}, u32[]{:S(2)}) collective-permute-start(bf16[8,128,128]{2,1,0:T(8,128)(2,1)S(1)} %get-tuple-element.42), channel_id=1, source_target_pairs={{0,2},{1,3},{2,0},{3,1},{4,6},{5,7},{6,4},{7,5},{8,10},{9,11},{10,... | collective-permute-start | bytes 786440 | tf_op jit(solution)/shard_map/ppermute | solution.py:336
  120.1 14.8 %collective-permute-start.27 = (bf16[8,128,128]{2,1,0:T(8,128)(2,1)S(1)}, bf16[8,128,128]{2,1,0:T(8,128)(2,1)S(1)}, u32[]{:S(2)}, u32[]{:S(2)}) collective-permute-start(bf16[8,128,128]{2,1,0:T(8,128)(2,1)S(1)} %get-tuple-element.43), channel_id=1, source_target_pairs={{0,3},{1,2},{2,1},{3,0},{4,7},{5,6},{6,5},{7,4},{8,11},{9,10},{10,... | collective-permute-start | bytes 786440 | tf_op jit(solution)/shard_map/ppermute | solution.py:336
  141.2 14.1 %collective-permute-start.30 = (bf16[8,128,128]{2,1,0:T(8,128)(2,1)}, bf16[8,128,128]{2,1,0:T(8,128)(2,1)}, u32[]{:S(2)}, u32[]{:S(2)}) collective-permute-start(bf16[8,128,128]{2,1,0:T(8,128)(2,1)} %get-tuple-element.65), channel_id=1, source_target_pairs={{0,24},{8,0},{16,8},{24,16},{1,25},{9,1},{17,9},{25,17},{2,26},{10... | collective-permute-start | bytes 786440 | tf_op jit(solution)/shard_map/ppermute | solution.py:266
  143.4 12.6 %collective-permute-start.29 = (bf16[8,128,128]{2,1,0:T(8,128)(2,1)}, bf16[8,128,128]{2,1,0:T(8,128)(2,1)}, u32[]{:S(2)}, u32[]{:S(2)}) collective-permute-start(bf16[8,128,128]{2,1,0:T(8,128)(2,1)} %get-tuple-element.66), channel_id=1, source_target_pairs={{0,16},{8,24},{16,0},{24,8},{1,17},{9,25},{17,1},{25,9},{2,18},{10... | collective-permute-start | bytes 786440 | tf_op jit(solution)/shard_map/ppermute | solution.py:266
  148.8 14.5 %collective-permute-start.13 = (bf16[256,1024]{1,0:T(8,128)(2,1)}, bf16[256,1024]{1,0:T(8,128)(2,1)}, u32[]{:S(2)}, u32[]{:S(2)}) collective-permute-start(bf16[256,1024]{1,0:T(8,128)(2,1)} %get-tuple-element.30), channel_id=1, source_target_pairs={{0,2},{2,0},{1,3},{3,1},{4,6},{6,4},{5,7},{7,5},{8,10},{10,8},{9,1... | collective-permute-start | bytes 1572872 | tf_op jit(solution)/shard_map/ppermute | solution.py:446
  165.5 12.3 %collective-permute-start.14 = (bf16[128,1024]{1,0:T(8,128)(2,1)}, bf16[128,1024]{1,0:T(8,128)(2,1)S(1)}, u32[]{:S(2)}, u32[]{:S(2)}) collective-permute-start(bf16[128,1024]{1,0:T(8,128)(2,1)} %fusion.70), channel_id=1, source_target_pairs={{0,4},{4,0},{1,5},{5,1},{2,6},{6,2},{3,7},{7,3},{8,12},{12,8},{9,1... | collective-permute-start | bytes 786440 | tf_op jit(solution)/shard_map/ppermute | solution.py:451
  (22 other events, 140.9 us)
where the time goes:
time: 181 us; the launch traced here: 180 us
  waiting for transfers between devices  68 us (38%)
  starting transfers between devices  53.1 us (29%)
  local copies, waits for them, and re-layouts  14.6 us (8%)
  Pallas kernels  14.6 us (8%)
  other arithmetic  14.2 us (8%)
  matrix products  13.8 us (8%)
    ppermute x12, waiting for transfers between devices, per_device(): received[slot] = lax.ppermute(passed, 'section', pairs)  36.7 us
    ppermute x12, starting transfers between devices, per_device(): received[slot] = lax.ppermute(passed, 'section', pairs)  18.2 us
    ppermute x4, starting transfers between devices, per_device(): pieces[sent] = lax.ppermute(after(held, passed), 'section', [(0, target)])  17.1 us
    dot_general x14, matrix products, per_device(): lax.dot_general(slope, layer_w, (((1,), (1,)), ((), ())), preferred_eleme...  13.8 us
    ppermute x9, waiting for transfers between devices, to_holders(): came.append(lax.ppermute(blocks[turn], ('near', 'core'), ways[turn]))  13.5 us
    ppermute x1, waiting for transfers between devices, per_device(): lax.ppermute(far_sum, 'far', [(0, 1), (1, 0)]).astype(jnp.float32)  8.15 us
    ppermute x9, starting transfers between devices, to_holders(): came.append(lax.ppermute(blocks[turn], ('near', 'core'), ways[turn]))  7.29 us
    ppermute x4, starting transfers between devices, exchange(): came = lax.ppermute(sent.astype(jnp.bfloat16), axis, turn)  7.13 us
  transfers between devices with their start and end apart: 32, of which 14 were waited for; matrix products, arithmetic and copies ran while one was open for 19% of the time, Pallas kernels for 8%

commit v1 on v0

--- a/solution.py
+++ b/solution.py
@@ -125,7 +125,7 @@
         in_specs=[
             pl.BlockSpec(
                 (1, in_group, 1, rows, hidden),
-                lambda c: (c // sections, 0, sections - 1 - c % sections, 0, 0),
+                lambda c: (c % groups, 0, sections - 1 - c // groups, 0, 0),
             )
         ],
         out_specs=pl.BlockSpec((hidden, in_group * rows), lambda c: (0, c)),
@@ -268,6 +268,19 @@
     return total
 
 
+def links_at(slot, sections):
+    last = sections - 1
+    chunk_count = GROUPS * sections
+    pairs = []
+    for section in range(1, sections):
+        if 0 <= slot - STREAMS * (last - section) < chunk_count:
+            pairs.append((section, section - 1))
+    chunk = slot - STREAMS * last
+    if 0 <= chunk and last - chunk // GROUPS > 0:
+        pairs.append((0, last - chunk // GROUPS))
+    return pairs
+
+
 def after(value, *others):
     return lax.optimization_barrier((value,) + others)[0]
 
@@ -294,14 +307,12 @@
     layer_w = weights[0]
 
     in_group = micro_count // GROUPS
-    order = list(range(last, -1, -1))
     chunk_count = GROUPS * sections
     chunk_rows = in_group * quarter
     view = (GROUPS, in_group, sections, quarter, hidden)
     cot_view = cotangent.reshape(view)
     pre_view = preact[0].reshape(view)
 
-    down = [(i, i - 1) for i in range(1, sections)]
     fill = STREAMS * last
     total_slots = chunk_count + fill
     shifts = [STREAMS * (last - pos) for pos in range(sections)]
@@ -338,8 +349,6 @@
 
     received = {}
     slopes = []
-    pieces = {}
-    waiting = []
     arrived = []
     ids = None
     for slot in range(total_slots):
@@ -349,37 +358,25 @@
             pre_view = after(pre_view, passed)
         pre_now = lax.dynamic_slice(
             pre_view,
-            (lax.div(spot, sections), zero, last - lax.rem(spot, sections), zero, zero),
+            (lax.rem(spot, GROUPS), zero, last - lax.div(spot, GROUPS), zero, zero),
             (1, in_group, 1, quarter, hidden),
         ).reshape(chunk_rows, hidden)
         if slot < chunk_count:
-            incoming = cot_view[slot // sections, :, order[slot % sections]]
+            incoming = cot_view[slot % GROUPS, :, last - slot // GROUPS]
             incoming = incoming.reshape(chunk_rows, hidden)
             if slot >= STREAMS:
-                incoming = jnp.where(is_last, incoming, received.pop(slot - STREAMS))
+                incoming = jnp.where(is_last, incoming, received[slot - STREAMS])
         else:
-            incoming = received.pop(slot - STREAMS)
+            incoming = received[slot - STREAMS]
         slope = jnp.where(pre_now > 0, incoming, jnp.zeros_like(incoming))
         slopes.append(slope)
         passed = lax.dot_general(
             slope, layer_w, (((1,), (1,)), ((), ())), preferred_element_type=jnp.float32
         ).astype(jnp.bfloat16)
-        chunk = slot - fill
-        target = order[chunk % sections] if chunk >= 0 else None
-        in_chain = slot < total_slots - STREAMS
-        if in_chain:
-            pairs = down + [(0, last)] if target == last else down
+        pairs = links_at(slot, sections)
+        if pairs:
             received[slot] = lax.ppermute(passed, "section", pairs)
-        if chunk >= 0:
-            if target == last and in_chain:
-                pieces[chunk] = received[slot]
-            elif target == 0:
-                pieces[chunk] = passed
-            else:
-                waiting.append((chunk, target, slot, passed))
-        if in_chain and slot % STREAMS != STREAMS - 1:
-            continue
-        if ids is None and slot > STREAMS:
+        if slot == 2 * STREAMS - 1:
             ids = jnp.transpose(after(row_ids, passed), (2, 0, 1))
             ids = jnp.repeat(ids.reshape(features, micro_count * quarter), row_split, axis=0)
             ids = ids.reshape(fars, group_size, slot_count, micro_count * quarter)
@@ -401,29 +398,19 @@
             if row_split > 1:
                 ids = ids - ((held_slots % row_split) * TROWS)[:, None]
             ids = ids[:, None, :]
-        elif ids is not None and flipped is None and unit % 128 == 0 and fars == nears == cores == 2:
+        if slot == 3 * STREAMS - 1 and unit % 128 == 0 and fars == nears == cores == 2:
             flipped = flip(after(in_view, passed))
-        ready = None
-        if chunk >= 0:
-            group = chunk // sections - (0 if chunk % sections == last else 1)
-            if group >= 0 and all(group * sections + q in pieces for q in range(sections)):
-                ready = group
-        for sent, target, sent_slot, held in waiting:
-            pieces[sent] = lax.ppermute(after(held, passed), "section", [(0, target)])
-        waiting = []
-        final = chunk == chunk_count - 1
-        if final:
-            ready = GROUPS - 1
-        if ready is None:
+        group = slot - (total_slots - GROUPS)
+        if group < 0:
             continue
-        ready_pieces = [pieces.pop(ready * sections + q) for q in range(sections)]
+        pieces = [received[fill + GROUPS * (last - q) + group] for q in range(last, 0, -1)]
         where = jnp.stack([section_pos] + partners).astype(jnp.int32)
         blocks = pair_grads(
             where,
-            ready_pieces,
-            order,
+            pieces + [passed],
+            list(range(last, -1, -1)),
             embeddings,
-            ready,
+            group,
             features * row_split,
             slot_count,
             group_size,
@@ -449,7 +436,7 @@
     if flipped is not None:
         far_sum = (far_rows + near_came[unit:]).astype(jnp.bfloat16)
         far_came = lax.ppermute(far_sum, "far", [(0, 1), (1, 0)]).astype(jnp.float32)
-        weight_grad = (own_rows + near_came[:unit] + far_came) * grad_scale
+        weight_grad = ((own_rows + near_came[:unit] + far_came) * grad_scale)[None]
     else:
         line = jnp.concatenate(slopes, 0)
         flat_slope = lax.dynamic_slice_in_dim(
@@ -458,8 +445,8 @@
             micro_count * batch_rows,
             0,
         )
-        in_order = in_view[:, :, jnp.asarray(order)]
-        in_order = jnp.swapaxes(in_order, 1, 2).reshape(micro_count * batch_rows, hidden)
+        in_order = jnp.transpose(in_view[:, :, ::-1], (2, 0, 1, 3, 4))
+        in_order = in_order.reshape(micro_count * batch_rows, hidden)
         full = lax.dot_general(
             in_order, flat_slope, (((0,), (0,)), ((), ())), preferred_element_type=jnp.float32
         ).reshape(stacks, cores, unit, hidden)
@@ -469,13 +456,13 @@
             turn = [(i, (i + shift) % cores) for i in range(cores)]
             came = lax.ppermute(side.astype(jnp.bfloat16), "core", turn)
             summed = summed + came.astype(jnp.float32)
-        weight_grad = exchange(summed, ("far", "near")) * grad_scale
+        weight_grad = (exchange(summed, ("far", "near")) * grad_scale)[None]
 
     table = exchange(table, "section")
     table = table.reshape(fars, slot_count, TROWS // sections, emb_width)
     table_grad = exchange(table, "far")
     table_grad = table_grad * grad_scale
-    return (weight_grad[None], table_grad)
+    return (weight_grad, table_grad)
 
 
 def solution(mesh):

time: 181 us -> 168 us (0.928)
  starting transfers between devices: 53.1 us -> 43.1 us
  waiting for transfers between devices: 68 us -> 65.2 us
    ppermute x4 -> x0, starting transfers between devices: 17.1 us -> none  [per_device(): pieces[sent] = lax.ppermute(after(held, passed), 'section', [(0, target)])]
    ppermute x12, starting transfers between devices: 18.2 us -> 26 us  [per_device(): received[slot] = lax.ppermute(passed, 'section', pairs)]
    ppermute x12, waiting for transfers between devices: 36.7 us -> 31 us  [per_device(): received[slot] = lax.ppermute(passed, 'section', pairs)]
    ppermute x9, waiting for transfers between devices: 13.5 us -> 15.7 us  [to_holders(): came.append(lax.ppermute(blocks[turn], ('near', 'core'), ways[turn]))]
  transfers between devices with their start and end apart: 32 -> 28, of which waited for: 14 -> 16; matrix products, arithmetic and copies ran while one was open for 19% -> 21% of each run, Pallas kernels for 8% -> 9%
where the time goes in v1:
time: 168 us; the launch traced here: 167 us
  waiting for transfers between devices  65.2 us (39%)
  starting transfers between devices  43.1 us (26%)
  Pallas kernels  14.6 us (9%)
  local copies, waits for them, and re-layouts  14.5 us (9%)
  other arithmetic  14.2 us (8%)
  matrix products  13.7 us (8%)
    ppermute x12, waiting for transfers between devices, per_device(): received[slot] = lax.ppermute(passed, 'section', pairs)  31 us
    ppermute x12, starting transfers between devices, per_device(): received[slot] = lax.ppermute(passed, 'section', pairs)  26 us
    ppermute x9, waiting for transfers between devices, to_holders(): came.append(lax.ppermute(blocks[turn], ('near', 'core'), ways[turn]))  15.7 us
    dot_general x14, matrix products, per_device(): lax.dot_general(slope, layer_w, (((1,), (1,)), ((), ())), preferred_eleme...  13.7 us
    ppermute x1, waiting for transfers between devices, per_device(): lax.ppermute(far_sum, 'far', [(0, 1), (1, 0)]).astype(jnp.float32)  8.76 us
    ppermute x9, starting transfers between devices, to_holders(): came.append(lax.ppermute(blocks[turn], ('near', 'core'), ways[turn]))  7.09 us
    ppermute x4, waiting for transfers between devices, exchange(): came = lax.ppermute(sent.astype(jnp.bfloat16), axis, turn)  7.03 us
    ppermute x4, starting transfers between devices, exchange(): came = lax.ppermute(sent.astype(jnp.bfloat16), axis, turn)  5.58 us
  transfers between devices with their start and end apart: 28, of which 16 were waited for; matrix products, arithmetic and copies ran while one was open for 21% of the time, Pallas kernels for 9%

profile of v1, /device:TPU:0, one launch (start us, length us, event | category | flops | bytes accessed | tf_op | source)
XLA Modules:
  0.0 166.8 jit_solution(11060584050025488958)
XLA Ops:
  9.2 2.3 %fusion.78 = (bf16[1,2,1,64,1024]{4,3,2,1,0:T(8,128)(2,1)S(1)}, bf16[1,2,1,64,1024]{4,3,2,1,0:T(8,128)(2,1)S(1)}, bf16[1,2,1,64,1024]{4,3,2,1,0:T(8,128)(2,1)}, ...) fusion(bf16[2,2,4,64,1024]{4,3,2,1,0:T(8,128)(2,1)} %bitcast.194), kind=kLoop, calls=%fused_computation.106 | loop fusion | bytes 3145728 | tf_op jit(solution)/shard_map/slice | solution.py:365
  24.6 2.6 %collective-permute-start.16 = (s32[8,256]{1,0:T(8,128)}, s32[8,256]{1,0:T(8,128)S(1)}, u32[]{:S(2)}, u32[]{:S(2)}) collective-permute-start(s32[8,256]{1,0:T(8,128)} %reshape.80), channel_id=1, source_target_pairs={{0,2},{1,3},{2,0},{3,1},{4,6},{5,7},{6,4},{7,5},{8,10},{9,11},{10,... | collective-permute-start | bytes 24584 | tf_op jit(solution)/shard_map/ppermute | solution.py:347
  38.0 22.3 %collective-permute-done.4 = bf16[128,1024]{1,0:T(8,128)(2,1)S(1)} collective-permute-done((bf16[128,1024]{1,0:T(8,128)(2,1)S(1)}, bf16[128,1024]{1,0:T(8,128)(2,1)S(1)}, u32[]{:S(2)}, u32[]{:S(2)}) %collective-permute-start.4) | collective-permute-done | bytes 262176 | tf_op jit(solution)/shard_map/ppermute | solution.py:378
  62.8 3.1 %collective-permute-done.5 = bf16[128,1024]{1,0:T(8,128)(2,1)S(1)} collective-permute-done((bf16[128,1024]{1,0:T(8,128)(2,1)S(1)}, bf16[128,1024]{1,0:T(8,128)(2,1)S(1)}, u32[]{:S(2)}, u32[]{:S(2)}) %collective-permute-start.5) | collective-permute-done | bytes 262176 | tf_op jit(solution)/shard_map/ppermute | solution.py:378
  68.4 3.1 %collective-permute-done.6.rest_0_ = bf16[128,1024]{1,0:T(8,128)(2,1)S(1)} collective-permute-done((bf16[128,1024]{1,0:T(8,128)(2,1)S(1)}, bf16[128,1024]{1,0:T(8,128)(2,1)S(1)}, u32[]{:S(2)}, u32[]{:S(2)}) %collective-permute-start.6) | collective-permute-done | bytes 262176 | tf_op jit(solution)/shard_map/ppermute | solution.py:378
  72.4 4.3 %collective-permute-start.8 = (bf16[128,1024]{1,0:T(8,128)(2,1)S(1)}, bf16[128,1024]{1,0:T(8,128)(2,1)S(1)}, u32[]{:S(2)}, u32[]{:S(2)}) collective-permute-start(bf16[128,1024]{1,0:T(8,128)(2,1)S(1)} %fusion.55), channel_id=1, source_target_pairs={{8,0},{16,8},{0,16},{9,1},{17,9},{1,17},{10,2},{18,10},{2,18},{11,... | collective-permute-start | bytes 786440 | tf_op jit(solution)/shard_map/ppermute | solution.py:378
  77.6 3.8 %collective-permute-start.9 = (bf16[128,1024]{1,0:T(8,128)(2,1)S(1)}, bf16[128,1024]{1,0:T(8,128)(2,1)S(1)}, u32[]{:S(2)}, u32[]{:S(2)}) collective-permute-start(bf16[128,1024]{1,0:T(8,128)(2,1)S(1)} %fusion.52), channel_id=1, source_target_pairs={{8,0},{16,8},{0,16},{9,1},{17,9},{1,17},{10,2},{18,10},{2,18},{11,... | collective-permute-start | bytes 786440 | tf_op jit(solution)/shard_map/ppermute | solution.py:378
  83.1 4.7 %collective-permute-start.10 = (bf16[128,1024]{1,0:T(8,128)(2,1)S(1)}, bf16[128,1024]{1,0:T(8,128)(2,1)S(1)}, u32[]{:S(2)}, u32[]{:S(2)}) collective-permute-start(bf16[128,1024]{1,0:T(8,128)(2,1)S(1)} %fusion.61), channel_id=1, source_target_pairs={{8,0},{0,8},{9,1},{1,9},{10,2},{2,10},{11,3},{3,11},{12,4},{4,12},... | collective-permute-start | bytes 786440 | tf_op jit(solution)/shard_map/ppermute | solution.py:378
  90.1 3.1 %collective-permute-start.11 = (bf16[128,1024]{1,0:T(8,128)(2,1)S(1)}, bf16[128,1024]{1,0:T(8,128)(2,1)S(1)}, u32[]{:S(2)}, u32[]{:S(2)}) collective-permute-start(bf16[128,1024]{1,0:T(8,128)(2,1)S(1)} %fusion.58), channel_id=1, source_target_pairs={{8,0},{0,8},{9,1},{1,9},{10,2},{2,10},{11,3},{3,11},{12,4},{4,12},... | collective-permute-start | bytes 786440 | tf_op jit(solution)/shard_map/ppermute | solution.py:378
  94.9 2.0 %pair_grads.2 = (bf16[8,128,128]{2,1,0:T(8,128)(2,1)S(1)}, bf16[8,128,128]{2,1,0:T(8,128)(2,1)S(1)}, bf16[8,128,128]{2,1,0:T(8,128)(2,1)S(1)}, bf16[8,128,128]{2,1,0:T(8,128)(2,1)S(1)}) custom-call(s32[5]{0:T(128)S(1)} %stack.52.where_ref, bf16[128,1024]{1,0:T(8,128)(2,1)S(1)} %collective-permute-done.6.rest_0_, ...), custom_call_target="tpu_custom_call" | custom-call | flops 268435456 | bytes 3145728 | tf_op jit(solution)/shard_map/pair_grads/pallas_call | solution.py:56
  98.9 2.2 %weight_half.2 = bf16[512,1024]{1,0:T(8,128)(2,1)S(1)} custom-call(s32[4]{0:T(128)S(1)} %pad_add_fusion.where_ref, bf16[1024,1024]{1,0:T(8,128)(2,1)S(1)} %flip.1.flipped_ref, bf16[128,1024]{1,0:T(8,128)(2,1)S(1)} %bitcast.180, bf16[128,1024]{1,0:T(8,128)(2,1)S(1)} %bitcast.183, bf16[128,1024]{1,0:T(8,128)(2,1)S(1)} %bitcast_select_fusion.9.rest_2_, ...), custom_call_target="tpu_custom_call" | custom-call | flops 1073741824 | bytes 6291456 | tf_op jit(solution)/shard_map/weight_half/pallas_call | solution.py:227
  102.4 2.0 %pair_grads.3 = (bf16[8,128,128]{2,1,0:T(8,128)(2,1)S(1)}, bf16[8,128,128]{2,1,0:T(8,128)(2,1)S(1)}, bf16[8,128,128]{2,1,0:T(8,128)(2,1)S(1)}, bf16[8,128,128]{2,1,0:T(8,128)(2,1)S(1)}) custom-call(s32[5]{0:T(128)S(1)} %stack.52.where_ref, bf16[128,1024]{1,0:T(8,128)(2,1)S(1)} %collective-permute-done.7.rest_0_, ...), custom_call_target="tpu_custom_call" | custom-call | flops 268435456 | bytes 3145728 | tf_op jit(solution)/shard_map/pair_grads/pallas_call | solution.py:56
  106.5 4.5 %collective-permute-done.20.rest_3_ = bf16[8,128,128]{2,1,0:T(8,128)(2,1)S(1)} collective-permute-done((bf16[8,128,128]{2,1,0:T(8,128)(2,1)S(1)}, bf16[8,128,128]{2,1,0:T(8,128)(2,1)S(1)}, u32[]{:S(2)}, u32[]{:S(2)}) %collective-permute-start.20) | collective-permute-done | bytes 262176 | tf_op jit(solution)/shard_map/ppermute | solution.py:347
  111.0 6.5 %collective-permute-done.22.rest_6_ = bf16[8,128,128]{2,1,0:T(8,128)(2,1)S(1)} collective-permute-done((bf16[8,128,128]{2,1,0:T(8,128)(2,1)S(1)}, bf16[8,128,128]{2,1,0:T(8,128)(2,1)S(1)}, u32[]{:S(2)}, u32[]{:S(2)}) %collective-permute-start.22) | collective-permute-done | bytes 262176 | tf_op jit(solution)/shard_map/ppermute | solution.py:347
  117.5 4.5 %collective-permute-done.23.rest_7_ = bf16[8,128,128]{2,1,0:T(8,128)(2,1)S(1)} collective-permute-done((bf16[8,128,128]{2,1,0:T(8,128)(2,1)S(1)}, bf16[8,128,128]{2,1,0:T(8,128)(2,1)S(1)}, u32[]{:S(2)}, u32[]{:S(2)}) %collective-permute-start.23) | collective-permute-done | bytes 262176 | tf_op jit(solution)/shard_map/ppermute | solution.py:347
  122.1 3.7 %row_sums.1 = bf16[4,8,128,128]{3,2,1,0:T(8,128)(2,1)S(1)} custom-call(s32[8,1,1024]{2,1,0:T(1,128)S(1)} %broadcast_in_dim.7.ids_ref, bf16[8,128,128]{2,1,0:T(8,128)(2,1)S(1)} %get-tuple-element.30.rest_0_, bf16[8,128,128]{2,1,0:T(8,128)(2,1)S(1)} %collective-permute-done.18.rest_1_, bf16[8,128,128]{2,1,0:T(8,128)(2,1)S(1)} %collective-permute-done.19.rest_2_, ...), custom_call_target="tpu_custom_call" | custom-call | flops 1073741824 | bytes 3145728 | tf_op jit(solution)/shard_map/row_sums/pallas_call | solution.py:98
  128.3 2.3 %collective-permute-start.26 = (bf16[8,128,128]{2,1,0:T(8,128)(2,1)}, bf16[8,128,128]{2,1,0:T(8,128)(2,1)}, u32[]{:S(2)}, u32[]{:S(2)}) collective-permute-start(bf16[8,128,128]{2,1,0:T(8,128)(2,1)} %get-tuple-element.59), channel_id=1, source_target_pairs={{0,24},{8,0},{16,8},{24,16},{1,25},{9,1},{17,9},{25,17},{2,26},{10... | collective-permute-start | bytes 786440 | tf_op jit(solution)/shard_map/ppermute | solution.py:266
  130.6 3.0 %weight_half.3 = (f32[128,1024]{1,0:T(8,128)S(1)}, f32[128,1024]{1,0:T(8,128)S(1)}, bf16[256,1024]{1,0:T(8,128)(2,1)}) custom-call(s32[4]{0:T(128)S(1)} %pad_add_fusion.1.where_ref, bf16[1024,1024]{1,0:T(8,128)(2,1)S(1)} %flip.1.flipped_ref, bf16[128,1024]{1,0:T(8,128)(2,1)S(1)} %bitcast.181, bf16[128,1024]{1,0:T(8,128)(2,1)S(1)} %bitcast.184, ...), custom_call_target="tpu_custom_call" | custom-call | flops 1073741824 | bytes 6291456 | tf_op jit(solution)/shard_map/weight_half/pallas_call | solution.py:227
  136.0 2.1 %collective-permute-done.24 = bf16[8,128,128]{2,1,0:T(8,128)(2,1)} collective-permute-done((bf16[8,128,128]{2,1,0:T(8,128)(2,1)}, bf16[8,128,128]{2,1,0:T(8,128)(2,1)}, u32[]{:S(2)}, u32[]{:S(2)}) %collective-permute-start.24) | collective-permute-done | bytes 262176 | tf_op jit(solution)/shard_map/ppermute | solution.py:266
  138.1 3.0 %collective-permute-done.26 = bf16[8,128,128]{2,1,0:T(8,128)(2,1)} collective-permute-done((bf16[8,128,128]{2,1,0:T(8,128)(2,1)}, bf16[8,128,128]{2,1,0:T(8,128)(2,1)}, u32[]{:S(2)}, u32[]{:S(2)}) %collective-permute-start.26) | collective-permute-done | bytes 262176 | tf_op jit(solution)/shard_map/ppermute | solution.py:266
  144.4 2.7 %collective-permute-start.27 = (bf16[4,128,128]{2,1,0:T(8,128)(2,1)S(1)}, bf16[4,128,128]{2,1,0:T(8,128)(2,1)}, u32[]{:S(2)}, u32[]{:S(2)}) collective-permute-start(bf16[4,128,128]{2,1,0:T(8,128)(2,1)S(1)} %fusion.77), channel_id=1, source_target_pairs={{0,4},{4,0},{1,5},{5,1},{2,6},{6,2},{3,7},{7,3},{8,12},{12,8},{9,1... | collective-permute-start | bytes 393224 | tf_op jit(solution)/shard_map/ppermute | solution.py:266
  147.1 2.7 %collective-permute-done.13 = bf16[256,1024]{1,0:T(8,128)(2,1)} collective-permute-done((bf16[256,1024]{1,0:T(8,128)(2,1)}, bf16[256,1024]{1,0:T(8,128)(2,1)}, u32[]{:S(2)}, u32[]{:S(2)}) %collective-permute-start.13) | collective-permute-done | bytes 524320 | tf_op jit(solution)/shard_map/ppermute | solution.py:433
  151.9 2.4 %collective-permute-start.14 = (bf16[128,1024]{1,0:T(8,128)(2,1)}, bf16[128,1024]{1,0:T(8,128)(2,1)S(1)}, u32[]{:S(2)}, u32[]{:S(2)}) collective-permute-start(bf16[128,1024]{1,0:T(8,128)(2,1)} %fusion.70), channel_id=1, source_target_pairs={{0,4},{4,0},{1,5},{5,1},{2,6},{6,2},{3,7},{7,3},{8,12},{12,8},{9,1... | collective-permute-start | bytes 786440 | tf_op jit(solution)/shard_map/ppermute | solution.py:438
  156.1 8.8 %collective-permute-done.14 = bf16[128,1024]{1,0:T(8,128)(2,1)S(1)} collective-permute-done((bf16[128,1024]{1,0:T(8,128)(2,1)}, bf16[128,1024]{1,0:T(8,128)(2,1)S(1)}, u32[]{:S(2)}, u32[]{:S(2)}) %collective-permute-start.14) | collective-permute-done | bytes 262176 | tf_op jit(solution)/shard_map/ppermute | solution.py:438
  (126 shorter events, 64.0 us)
Async XLA Ops:
  4.1 23.2 %collective-permute-start.2 = (bf16[128,1024]{1,0:T(8,128)(2,1)}, bf16[128,1024]{1,0:T(8,128)(2,1)}, u32[]{:S(2)}, u32[]{:S(2)}) collective-permute-start(bf16[128,1024]{1,0:T(8,128)(2,1)} %fusion.37), channel_id=1, source_target_pairs={{24,16},{25,17},{26,18},{27,19},{28,20},{29,21},{30,22},{31,23}} | collective-permute-start | bytes 786440 | tf_op jit(solution)/shard_map/ppermute | solution.py:378
  14.7 18.1 %collective-permute-start.1 = (bf16[128,1024]{1,0:T(8,128)(2,1)}, bf16[128,1024]{1,0:T(8,128)(2,1)}, u32[]{:S(2)}, u32[]{:S(2)}) collective-permute-start(bf16[128,1024]{1,0:T(8,128)(2,1)} %fusion.31), channel_id=1, source_target_pairs={{16,8},{24,16},{17,9},{25,17},{18,10},{26,18},{19,11},{27,19},{20,... | collective-permute-start | bytes 786440 | tf_op jit(solution)/shard_map/ppermute | solution.py:378
  24.1 6.2 %collective-permute-start.15 = (s32[8,256]{1,0:T(8,128)}, s32[8,256]{1,0:T(8,128)S(1)}, u32[]{:S(2)}, u32[]{:S(2)}) collective-permute-start(s32[8,256]{1,0:T(8,128)} %reshape.79), channel_id=1, source_target_pairs={{0,1},{1,0},{2,3},{3,2},{4,5},{5,4},{6,7},{7,6},{8,9},{9,8},{10,11... | collective-permute-start | bytes 24584 | tf_op jit(solution)/shard_map/ppermute | solution.py:347
  31.4 28.9 %collective-permute-start.4 = (bf16[128,1024]{1,0:T(8,128)(2,1)S(1)}, bf16[128,1024]{1,0:T(8,128)(2,1)S(1)}, u32[]{:S(2)}, u32[]{:S(2)}) collective-permute-start(bf16[128,1024]{1,0:T(8,128)(2,1)S(1)} %fusion.43), channel_id=1, source_target_pairs={{8,0},{16,8},{24,16},{9,1},{17,9},{25,17},{10,2},{18,10},{26,18},{... | collective-permute-start | bytes 786440 | tf_op jit(solution)/shard_map/ppermute | solution.py:378
  34.7 31.2 %collective-permute-start.5 = (bf16[128,1024]{1,0:T(8,128)(2,1)S(1)}, bf16[128,1024]{1,0:T(8,128)(2,1)S(1)}, u32[]{:S(2)}, u32[]{:S(2)}) collective-permute-start(bf16[128,1024]{1,0:T(8,128)(2,1)S(1)} %fusion.34), channel_id=1, source_target_pairs={{8,0},{16,8},{24,16},{9,1},{17,9},{25,17},{10,2},{18,10},{26,18},{... | collective-permute-start | bytes 786440 | tf_op jit(solution)/shard_map/ppermute | solution.py:378
  61.2 10.3 %collective-permute-start.6 = (bf16[128,1024]{1,0:T(8,128)(2,1)S(1)}, bf16[128,1024]{1,0:T(8,128)(2,1)S(1)}, u32[]{:S(2)}, u32[]{:S(2)}) collective-permute-start(bf16[128,1024]{1,0:T(8,128)(2,1)S(1)} %fusion.49), channel_id=1, source_target_pairs={{8,0},{16,8},{24,16},{0,24},{9,1},{17,9},{25,17},{1,25},{10,2},{18... | collective-permute-start | bytes 786440 | tf_op jit(solution)/shard_map/ppermute | solution.py:378
  66.8 9.9 %collective-permute-start.7 = (bf16[128,1024]{1,0:T(8,128)(2,1)S(1)}, bf16[128,1024]{1,0:T(8,128)(2,1)S(1)}, u32[]{:S(2)}, u32[]{:S(2)}) collective-permute-start(bf16[128,1024]{1,0:T(8,128)(2,1)S(1)} %fusion.46), channel_id=1, source_target_pairs={{8,0},{16,8},{24,16},{0,24},{9,1},{17,9},{25,17},{1,25},{10,2},{18... | collective-permute-start | bytes 786440 | tf_op jit(solution)/shard_map/ppermute | solution.py:378
  72.4 9.9 %collective-permute-start.8 = (bf16[128,1024]{1,0:T(8,128)(2,1)S(1)}, bf16[128,1024]{1,0:T(8,128)(2,1)S(1)}, u32[]{:S(2)}, u32[]{:S(2)}) collective-permute-start(bf16[128,1024]{1,0:T(8,128)(2,1)S(1)} %fusion.55), channel_id=1, source_target_pairs={{8,0},{16,8},{0,16},{9,1},{17,9},{1,17},{10,2},{18,10},{2,18},{11,... | collective-permute-start | bytes 786440 | tf_op jit(solution)/shard_map/ppermute | solution.py:378
  77.6 11.6 %collective-permute-start.9 = (bf16[128,1024]{1,0:T(8,128)(2,1)S(1)}, bf16[128,1024]{1,0:T(8,128)(2,1)S(1)}, u32[]{:S(2)}, u32[]{:S(2)}) collective-permute-start(bf16[128,1024]{1,0:T(8,128)(2,1)S(1)} %fusion.52), channel_id=1, source_target_pairs={{8,0},{16,8},{0,16},{9,1},{17,9},{1,17},{10,2},{18,10},{2,18},{11,... | collective-permute-start | bytes 786440 | tf_op jit(solution)/shard_map/ppermute | solution.py:378
  83.1 10.9 %collective-permute-start.10 = (bf16[128,1024]{1,0:T(8,128)(2,1)S(1)}, bf16[128,1024]{1,0:T(8,128)(2,1)S(1)}, u32[]{:S(2)}, u32[]{:S(2)}) collective-permute-start(bf16[128,1024]{1,0:T(8,128)(2,1)S(1)} %fusion.61), channel_id=1, source_target_pairs={{8,0},{0,8},{9,1},{1,9},{10,2},{2,10},{11,3},{3,11},{12,4},{4,12},... | collective-permute-start | bytes 786440 | tf_op jit(solution)/shard_map/ppermute | solution.py:378
  90.1 8.8 %collective-permute-start.11 = (bf16[128,1024]{1,0:T(8,128)(2,1)S(1)}, bf16[128,1024]{1,0:T(8,128)(2,1)S(1)}, u32[]{:S(2)}, u32[]{:S(2)}) collective-permute-start(bf16[128,1024]{1,0:T(8,128)(2,1)S(1)} %fusion.58), channel_id=1, source_target_pairs={{8,0},{0,8},{9,1},{1,9},{10,2},{2,10},{11,3},{3,11},{12,4},{4,12},... | collective-permute-start | bytes 786440 | tf_op jit(solution)/shard_map/ppermute | solution.py:378
  97.0 7.6 %collective-permute-start.18 = (bf16[8,128,128]{2,1,0:T(8,128)(2,1)S(1)}, bf16[8,128,128]{2,1,0:T(8,128)(2,1)S(1)}, u32[]{:S(2)}, u32[]{:S(2)}) collective-permute-start(bf16[8,128,128]{2,1,0:T(8,128)(2,1)S(1)} %get-tuple-element.31), channel_id=1, source_target_pairs={{0,1},{1,0},{2,3},{3,2},{4,5},{5,4},{6,7},{7,6},{8,9},{9,8},{10,11... | collective-permute-start | bytes 786440 | tf_op jit(solution)/shard_map/ppermute | solution.py:347
  97.0 9.2 %collective-permute-start.19 = (bf16[8,128,128]{2,1,0:T(8,128)(2,1)S(1)}, bf16[8,128,128]{2,1,0:T(8,128)(2,1)S(1)}, u32[]{:S(2)}, u32[]{:S(2)}) collective-permute-start(bf16[8,128,128]{2,1,0:T(8,128)(2,1)S(1)} %get-tuple-element.32), channel_id=1, source_target_pairs={{0,2},{1,3},{2,0},{3,1},{4,6},{5,7},{6,4},{7,5},{8,10},{9,11},{10,... | collective-permute-start | bytes 786440 | tf_op jit(solution)/shard_map/ppermute | solution.py:347
  98.7 12.3 %collective-permute-start.20 = (bf16[8,128,128]{2,1,0:T(8,128)(2,1)S(1)}, bf16[8,128,128]{2,1,0:T(8,128)(2,1)S(1)}, u32[]{:S(2)}, u32[]{:S(2)}) collective-permute-start(bf16[8,128,128]{2,1,0:T(8,128)(2,1)S(1)} %get-tuple-element.33), channel_id=1, source_target_pairs={{0,3},{1,2},{2,1},{3,0},{4,7},{5,6},{6,5},{7,4},{8,11},{9,10},{10,... | collective-permute-start | bytes 786440 | tf_op jit(solution)/shard_map/ppermute | solution.py:347
  101.1 29.5 %collective-permute-start.12 = (bf16[512,1024]{1,0:T(8,128)(2,1)S(1)}, bf16[512,1024]{1,0:T(8,128)(2,1)S(1)}, u32[]{:S(2)}, u32[]{:S(2)}) collective-permute-start(bf16[512,1024]{1,0:T(8,128)(2,1)S(1)} %weight_half.2), channel_id=1, source_target_pairs={{0,1},{1,0},{2,3},{3,2},{4,5},{5,4},{6,7},{7,6},{8,9},{9,8},{10,11... | collective-permute-start | bytes 3145736 | tf_op jit(solution)/shard_map/ppermute | solution.py:426
  104.4 6.6 %collective-permute-start.21 = (bf16[8,128,128]{2,1,0:T(8,128)(2,1)S(1)}, bf16[8,128,128]{2,1,0:T(8,128)(2,1)S(1)}, u32[]{:S(2)}, u32[]{:S(2)}) collective-permute-start(bf16[8,128,128]{2,1,0:T(8,128)(2,1)S(1)} %get-tuple-element.35), channel_id=1, source_target_pairs={{0,1},{1,0},{2,3},{3,2},{4,5},{5,4},{6,7},{7,6},{8,9},{9,8},{10,11... | collective-permute-start | bytes 786440 | tf_op jit(solution)/shard_map/ppermute | solution.py:347
  104.6 12.9 %collective-permute-start.22 = (bf16[8,128,128]{2,1,0:T(8,128)(2,1)S(1)}, bf16[8,128,128]{2,1,0:T(8,128)(2,1)S(1)}, u32[]{:S(2)}, u32[]{:S(2)}) collective-permute-start(bf16[8,128,128]{2,1,0:T(8,128)(2,1)S(1)} %get-tuple-element.36), channel_id=1, source_target_pairs={{0,2},{1,3},{2,0},{3,1},{4,6},{5,7},{6,4},{7,5},{8,10},{9,11},{10,... | collective-permute-start | bytes 786440 | tf_op jit(solution)/shard_map/ppermute | solution.py:347
  106.3 15.8 %collective-permute-start.23 = (bf16[8,128,128]{2,1,0:T(8,128)(2,1)S(1)}, bf16[8,128,128]{2,1,0:T(8,128)(2,1)S(1)}, u32[]{:S(2)}, u32[]{:S(2)}) collective-permute-start(bf16[8,128,128]{2,1,0:T(8,128)(2,1)S(1)} %get-tuple-element.37), channel_id=1, source_target_pairs={{0,3},{1,2},{2,1},{3,0},{4,7},{5,6},{6,5},{7,4},{8,11},{9,10},{10,... | collective-permute-start | bytes 786440 | tf_op jit(solution)/shard_map/ppermute | solution.py:347
  127.6 10.4 %collective-permute-start.24 = (bf16[8,128,128]{2,1,0:T(8,128)(2,1)}, bf16[8,128,128]{2,1,0:T(8,128)(2,1)}, u32[]{:S(2)}, u32[]{:S(2)}) collective-permute-start(bf16[8,128,128]{2,1,0:T(8,128)(2,1)} %get-tuple-element.58), channel_id=1, source_target_pairs={{0,8},{8,16},{16,24},{24,0},{1,9},{9,17},{17,25},{25,1},{2,10},{10... | collective-permute-start | bytes 786440 | tf_op jit(solution)/shard_map/ppermute | solution.py:266
  128.3 12.8 %collective-permute-start.26 = (bf16[8,128,128]{2,1,0:T(8,128)(2,1)}, bf16[8,128,128]{2,1,0:T(8,128)(2,1)}, u32[]{:S(2)}, u32[]{:S(2)}) collective-permute-start(bf16[8,128,128]{2,1,0:T(8,128)(2,1)} %get-tuple-element.59), channel_id=1, source_target_pairs={{0,24},{8,0},{16,8},{24,16},{1,25},{9,1},{17,9},{25,17},{2,26},{10... | collective-permute-start | bytes 786440 | tf_op jit(solution)/shard_map/ppermute | solution.py:266
  130.6 12.5 %collective-permute-start.25 = (bf16[8,128,128]{2,1,0:T(8,128)(2,1)}, bf16[8,128,128]{2,1,0:T(8,128)(2,1)}, u32[]{:S(2)}, u32[]{:S(2)}) collective-permute-start(bf16[8,128,128]{2,1,0:T(8,128)(2,1)} %get-tuple-element.60), channel_id=1, source_target_pairs={{0,16},{8,24},{16,0},{24,8},{1,17},{9,25},{17,1},{25,9},{2,18},{10... | collective-permute-start | bytes 786440 | tf_op jit(solution)/shard_map/ppermute | solution.py:266
  134.4 15.3 %collective-permute-start.13 = (bf16[256,1024]{1,0:T(8,128)(2,1)}, bf16[256,1024]{1,0:T(8,128)(2,1)}, u32[]{:S(2)}, u32[]{:S(2)}) collective-permute-start(bf16[256,1024]{1,0:T(8,128)(2,1)} %get-tuple-element.27), channel_id=1, source_target_pairs={{0,2},{2,0},{1,3},{3,1},{4,6},{6,4},{5,7},{7,5},{8,10},{10,8},{9,1... | collective-permute-start | bytes 1572872 | tf_op jit(solution)/shard_map/ppermute | solution.py:433
  144.4 10.0 %collective-permute-start.27 = (bf16[4,128,128]{2,1,0:T(8,128)(2,1)S(1)}, bf16[4,128,128]{2,1,0:T(8,128)(2,1)}, u32[]{:S(2)}, u32[]{:S(2)}) collective-permute-start(bf16[4,128,128]{2,1,0:T(8,128)(2,1)S(1)} %fusion.77), channel_id=1, source_target_pairs={{0,4},{4,0},{1,5},{5,1},{2,6},{6,2},{3,7},{7,3},{8,12},{12,8},{9,1... | collective-permute-start | bytes 393224 | tf_op jit(solution)/shard_map/ppermute | solution.py:266
  151.9 12.9 %collective-permute-start.14 = (bf16[128,1024]{1,0:T(8,128)(2,1)}, bf16[128,1024]{1,0:T(8,128)(2,1)S(1)}, u32[]{:S(2)}, u32[]{:S(2)}) collective-permute-start(bf16[128,1024]{1,0:T(8,128)(2,1)} %fusion.70), channel_id=1, source_target_pairs={{0,4},{4,0},{1,5},{5,1},{2,6},{6,2},{3,7},{7,3},{8,12},{12,8},{9,1... | collective-permute-start | bytes 786440 | tf_op jit(solution)/shard_map/ppermute | solution.py:438
  (18 other events, 69.2 us)

commit v2 on v1

--- a/solution.py
+++ b/solution.py
@@ -74,7 +74,7 @@
     )(where, *pieces, embeddings)
 
 
-def row_sums_body(ids_ref, *rest, rows):
+def row_sums_body(where_ref, ids_ref, *rest, rows):
     arrived_refs, out_ref = rest[:-1], rest[-1]
     width = arrived_refs[0].shape[1]
     sources = len(arrived_refs)
@@ -90,16 +90,23 @@
     out_ref[:, 0] = total.astype(out_ref.dtype).reshape(out_ref.shape[0], -1, total.shape[1])
 
 
-def row_sums(ids, arrived, rows, parts):
-    slots, width, emb = arrived[0].shape
+def row_sums(first, slots, ids, arrived, rows, parts):
+    _, width, emb = arrived[0].shape
     sources = len(arrived)
-    in_specs = [pl.BlockSpec((1, 1, sources * width), lambda s: (s, 0, 0))]
-    in_specs += [pl.BlockSpec((1, width, emb), lambda s: (s, 0, 0))] * sources
+
+    def held(s, where):
+        return (where[0] + s, 0, 0)
+
+    grid_spec = pltpu.PrefetchScalarGridSpec(
+        num_scalar_prefetch=1,
+        grid=(slots,),
+        in_specs=[pl.BlockSpec((1, 1, sources * width), held)]
+        + [pl.BlockSpec((1, width, emb), held)] * sources,
+        out_specs=pl.BlockSpec((parts, 1, rows // parts, emb), lambda s, where: (0, s, 0, 0)),
+    )
     return pl.pallas_call(
         functools.partial(row_sums_body, rows=rows),
-        grid=(slots,),
-        in_specs=in_specs,
-        out_specs=pl.BlockSpec((parts, 1, rows // parts, emb), lambda s: (0, s, 0, 0)),
+        grid_spec=grid_spec,
         out_shape=jax.ShapeDtypeStruct((parts, slots, rows // parts, emb), jnp.bfloat16),
         compiler_params=pltpu.CompilerParams(vmem_limit_bytes=16 * 2**20),
         cost_estimate=pl.CostEstimate(
@@ -108,7 +115,7 @@
             transcendentals=0,
         ),
         name="row_sums",
-    )(ids, *arrived)
+    )(jnp.reshape(first, (1,)).astype(jnp.int32), ids, *arrived)
 
 
 def flip_body(in_ref, out_ref):
@@ -208,11 +215,8 @@
     else:
         in_specs.append(pl.BlockSpec(came.shape, lambda i, where: (0, 0)))
         args.append(came)
-        shapes = [
-            jax.ShapeDtypeStruct((unit, hidden), jnp.float32),
-            jax.ShapeDtypeStruct((unit, hidden), jnp.float32),
-            jax.ShapeDtypeStruct((2 * unit, hidden), jnp.bfloat16),
-        ]
+        shapes = [jax.ShapeDtypeStruct((unit, hidden), jnp.float32)]
+        shapes += [jax.ShapeDtypeStruct((unit, hidden), jnp.bfloat16)] * (stacks - 1)
     grid_spec = pltpu.PrefetchScalarGridSpec(
         num_scalar_prefetch=1,
         grid=(1,),
@@ -350,7 +354,6 @@
     received = {}
     slopes = []
     arrived = []
-    ids = None
     for slot in range(total_slots):
         spot = jnp.clip(slot - shift_now, 0, chunk_count - 1)
         zero = jnp.zeros_like(spot)
@@ -376,29 +379,7 @@
         pairs = links_at(slot, sections)
         if pairs:
             received[slot] = lax.ppermute(passed, "section", pairs)
-        if slot == 2 * STREAMS - 1:
-            ids = jnp.transpose(after(row_ids, passed), (2, 0, 1))
-            ids = jnp.repeat(ids.reshape(features, micro_count * quarter), row_split, axis=0)
-            ids = ids.reshape(fars, group_size, slot_count, micro_count * quarter)
-            ids = [
-                lax.dynamic_index_in_dim(ids, partner, 1, False).reshape(
-                    fars * slot_count, micro_count * quarter
-                )
-                for partner in partners
-            ]
-            ids = to_holders(ids)
-            ids = jnp.concatenate(
-                [
-                    source[:, group * chunk_rows : (group + 1) * chunk_rows]
-                    for group in range(GROUPS)
-                    for source in ids
-                ],
-                axis=1,
-            )
-            if row_split > 1:
-                ids = ids - ((held_slots % row_split) * TROWS)[:, None]
-            ids = ids[:, None, :]
-        if slot == 3 * STREAMS - 1 and unit % 128 == 0 and fars == nears == cores == 2:
+        if slot == 2 * STREAMS - 1 and unit % 128 == 0 and fars == nears == cores == 2:
             flipped = flip(after(in_view, passed))
         group = slot - (total_slots - GROUPS)
         if group < 0:
@@ -418,6 +399,28 @@
         )
         arrived.append(to_holders(blocks))
 
+    ids = jnp.transpose(row_ids, (2, 0, 1))
+    ids = jnp.repeat(ids.reshape(features, micro_count * quarter), row_split, axis=0)
+    ids = ids.reshape(fars, group_size, slot_count, micro_count * quarter)
+    ids = [
+        lax.dynamic_index_in_dim(ids, partner, 1, False).reshape(
+            fars * slot_count, micro_count * quarter
+        )
+        for partner in partners
+    ]
+    ids = to_holders(ids)
+    ids = jnp.concatenate(
+        [
+            source[:, group * chunk_rows : (group + 1) * chunk_rows]
+            for group in range(GROUPS)
+            for source in ids
+        ],
+        axis=1,
+    )
+    if row_split > 1:
+        ids = ids - ((held_slots % row_split) * TROWS)[:, None]
+    ids = ids[:, None, :]
+
     if flipped is not None:
         where = jnp.stack(
             [section_pos, 1 - core_pos, stack_pos, jnp.full_like(section_pos, cores)]
@@ -427,16 +430,34 @@
         where = jnp.stack(
             [section_pos, core_pos, stack_pos, jnp.full_like(section_pos, cores)]
         ).astype(jnp.int32)
-        own_rows, far_rows, near_rows = weight_half(
-            where, flipped, slopes, shifts, stacks, from_own, came
-        )
-        near_came = lax.ppermute(near_rows, "near", [(0, 1), (1, 0)]).astype(jnp.float32)
-    table = row_sums(ids, [block for group in arrived for block in group], TROWS, sections)
+        own_rows, *other_rows = weight_half(where, flipped, slopes, shifts, stacks, from_own, came)
+        rows_came = []
+        for turn, block in enumerate(other_rows, 1):
+            way = [(i, from_own(i, turn)) for i in range(stacks)]
+            rows_came.append(lax.ppermute(block, ("far", "near"), way))
+    from_all = [block for group in arrived for block in group]
+    far_pos = lax.axis_index("far")
+    if fars == 2:
+        tables = []
+        for far in (1 - far_pos, far_pos):
+            tables.append(row_sums(far * slot_count, slot_count, ids, from_all, TROWS, sections))
+        other = exchange(tables[0], "section")
+        table = exchange(tables[1], "section")
+        crossed = lax.ppermute(other.astype(jnp.bfloat16), "far", [(0, 1), (1, 0)])
+        table_grad = (table + crossed.astype(jnp.float32)) * grad_scale
+    else:
+        table = row_sums(
+            jnp.zeros_like(far_pos), fars * slot_count, ids, from_all, TROWS, sections
+        )
+        table = exchange(table, "section")
+        table = table.reshape(fars, slot_count, TROWS // sections, emb_width)
+        table_grad = exchange(table, "far") * grad_scale
 
     if flipped is not None:
-        far_sum = (far_rows + near_came[unit:]).astype(jnp.bfloat16)
-        far_came = lax.ppermute(far_sum, "far", [(0, 1), (1, 0)]).astype(jnp.float32)
-        weight_grad = ((own_rows + near_came[:unit] + far_came) * grad_scale)[None]
+        weight_grad = own_rows
+        for block in rows_came:
+            weight_grad = weight_grad + block.astype(jnp.float32)
+        weight_grad = (weight_grad * grad_scale)[None]
     else:
         line = jnp.concatenate(slopes, 0)
         flat_slope = lax.dynamic_slice_in_dim(
@@ -458,10 +479,6 @@
             summed = summed + came.astype(jnp.float32)
         weight_grad = (exchange(summed, ("far", "near")) * grad_scale)[None]
 
-    table = exchange(table, "section")
-    table = table.reshape(fars, slot_count, TROWS // sections, emb_width)
-    table_grad = exchange(table, "far")
-    table_grad = table_grad * grad_scale
     return (weight_grad, table_grad)
 
 

time: 168 us -> 161 us (0.958)
  the two profiles are of different devices: /device:TPU:0 before, /device:TPU:19 now
where the time goes in v2:
time: 161 us
  waiting for transfers between devices  71.5 us (44%)
  starting transfers between devices  39.2 us (24%)
  Pallas kernels  13.9 us (9%)
  matrix products  13.2 us (8%)
  local copies, waits for them, and re-layouts  13.1 us (8%)
  other arithmetic  8.68 us (5%)
    ppermute x12, waiting for transfers between devices, per_device(): received[slot] = lax.ppermute(passed, 'section', pairs)  31.1 us
    ppermute x3, waiting for transfers between devices, per_device(): rows_came.append(lax.ppermute(block, ('far', 'near'), way))  24.7 us
    ppermute x12, starting transfers between devices, per_device(): received[slot] = lax.ppermute(passed, 'section', pairs)  17.5 us
    ppermute x9, waiting for transfers between devices, to_holders(): came.append(lax.ppermute(blocks[turn], ('near', 'core'), ways[turn]))  14.2 us
    dot_general x14, matrix products, per_device(): lax.dot_general(slope, layer_w, (((1,), (1,)), ((), ())), preferred_eleme...  13.2 us
    ppermute x9, starting transfers between devices, to_holders(): came.append(lax.ppermute(blocks[turn], ('near', 'core'), ways[turn]))  11.3 us
    unnamed x21, local copies, waits for them, and re-layouts  7.01 us
    ppermute x6, starting transfers between devices, exchange(): came = lax.ppermute(sent.astype(jnp.bfloat16), axis, turn)  6.47 us
  transfers between devices with their start and end apart: 32, of which 14 were waited for; matrix products, arithmetic and copies ran while one was open for 20% of the time, Pallas kernels for 9%

profile of v2, /device:TPU:19, one launch (start us, length us, event | category | flops | bytes accessed | tf_op | source)
XLA Modules:
  0.0 160.8 jit_solution(13318229220466424488)
XLA Ops:
  13.0 2.3 %fusion.77 = (bf16[1,2,1,64,1024]{4,3,2,1,0:T(8,128)(2,1)S(1)}, bf16[1,2,1,64,1024]{4,3,2,1,0:T(8,128)(2,1)S(1)}, bf16[1,2,1,64,1024]{4,3,2,1,0:T(8,128)(2,1)S(1...) fusion(bf16[2,2,4,64,1024]{4,3,2,1,0:T(8,128)(2,1)} %bitcast.198), kind=kLoop, calls=%fused_computation.106 | loop fusion | bytes 3145728 | tf_op jit(solution)/shard_map/slice | solution.py:368
  32.4 9.4 %collective-permute-done.2 = bf16[128,1024]{1,0:T(8,128)(2,1)S(1)} collective-permute-done((bf16[128,1024]{1,0:T(8,128)(2,1)S(1)}, bf16[128,1024]{1,0:T(8,128)(2,1)S(1)}, u32[]{:S(2)}, u32[]{:S(2)}) %collective-permute-start.2) | collective-permute-done | bytes 262176 | tf_op jit(solution)/shard_map/ppermute | solution.py:381
  42.7 1.9 %collective-permute-start.4 = (bf16[128,1024]{1,0:T(8,128)(2,1)S(1)}, bf16[128,1024]{1,0:T(8,128)(2,1)S(1)}, u32[]{:S(2)}, u32[]{:S(2)}) collective-permute-start(bf16[128,1024]{1,0:T(8,128)(2,1)S(1)} %fusion.43), channel_id=1, source_target_pairs={{8,0},{16,8},{24,16},{9,1},{17,9},{25,17},{10,2},{18,10},{26,18},{... | collective-permute-start | bytes 786440 | tf_op jit(solution)/shard_map/ppermute | solution.py:381
  45.6 1.9 %collective-permute-start.5 = (bf16[128,1024]{1,0:T(8,128)(2,1)S(1)}, bf16[128,1024]{1,0:T(8,128)(2,1)S(1)}, u32[]{:S(2)}, u32[]{:S(2)}) collective-permute-start(bf16[128,1024]{1,0:T(8,128)(2,1)S(1)} %fusion.40), channel_id=1, source_target_pairs={{8,0},{16,8},{24,16},{9,1},{17,9},{25,17},{10,2},{18,10},{26,18},{... | collective-permute-start | bytes 786440 | tf_op jit(solution)/shard_map/ppermute | solution.py:381
  47.7 4.6 %collective-permute-done.4 = bf16[128,1024]{1,0:T(8,128)(2,1)S(1)} collective-permute-done((bf16[128,1024]{1,0:T(8,128)(2,1)S(1)}, bf16[128,1024]{1,0:T(8,128)(2,1)S(1)}, u32[]{:S(2)}, u32[]{:S(2)}) %collective-permute-start.4) | collective-permute-done | bytes 262176 | tf_op jit(solution)/shard_map/ppermute | solution.py:381
  53.3 4.6 %collective-permute-done.5 = bf16[128,1024]{1,0:T(8,128)(2,1)S(1)} collective-permute-done((bf16[128,1024]{1,0:T(8,128)(2,1)S(1)}, bf16[128,1024]{1,0:T(8,128)(2,1)S(1)}, u32[]{:S(2)}, u32[]{:S(2)}) %collective-permute-start.5) | collective-permute-done | bytes 262176 | tf_op jit(solution)/shard_map/ppermute | solution.py:381
  59.1 4.4 %collective-permute-done.6.rest_0_ = bf16[128,1024]{1,0:T(8,128)(2,1)S(1)} collective-permute-done((bf16[128,1024]{1,0:T(8,128)(2,1)S(1)}, bf16[128,1024]{1,0:T(8,128)(2,1)S(1)}, u32[]{:S(2)}, u32[]{:S(2)}) %collective-permute-start.6) | collective-permute-done | bytes 262176 | tf_op jit(solution)/shard_map/ppermute | solution.py:381
  64.4 1.9 %collective-permute-start.8 = (bf16[128,1024]{1,0:T(8,128)(2,1)S(1)}, bf16[128,1024]{1,0:T(8,128)(2,1)S(1)}, u32[]{:S(2)}, u32[]{:S(2)}) collective-permute-start(bf16[128,1024]{1,0:T(8,128)(2,1)S(1)} %fusion.55), channel_id=1, source_target_pairs={{8,0},{16,8},{0,16},{9,1},{17,9},{1,17},{10,2},{18,10},{2,18},{11,... | collective-permute-start | bytes 786440 | tf_op jit(solution)/shard_map/ppermute | solution.py:381
  66.3 2.8 %collective-permute-done.7.rest_0_ = bf16[128,1024]{1,0:T(8,128)(2,1)S(1)} collective-permute-done((bf16[128,1024]{1,0:T(8,128)(2,1)S(1)}, bf16[128,1024]{1,0:T(8,128)(2,1)S(1)}, u32[]{:S(2)}, u32[]{:S(2)}) %collective-permute-start.7) | collective-permute-done | bytes 262176 | tf_op jit(solution)/shard_map/ppermute | solution.py:381
  70.0 1.9 %collective-permute-start.9 = (bf16[128,1024]{1,0:T(8,128)(2,1)S(1)}, bf16[128,1024]{1,0:T(8,128)(2,1)S(1)}, u32[]{:S(2)}, u32[]{:S(2)}) collective-permute-start(bf16[128,1024]{1,0:T(8,128)(2,1)S(1)} %fusion.52), channel_id=1, source_target_pairs={{8,0},{16,8},{0,16},{9,1},{17,9},{1,17},{10,2},{18,10},{2,18},{11,... | collective-permute-start | bytes 786440 | tf_op jit(solution)/shard_map/ppermute | solution.py:381
  76.0 4.2 %collective-permute-done.9.rest_1_ = bf16[128,1024]{1,0:T(8,128)(2,1)S(1)} collective-permute-done((bf16[128,1024]{1,0:T(8,128)(2,1)S(1)}, bf16[128,1024]{1,0:T(8,128)(2,1)S(1)}, u32[]{:S(2)}, u32[]{:S(2)}) %collective-permute-start.9) | collective-permute-done | bytes 262176 | tf_op jit(solution)/shard_map/ppermute | solution.py:381
  81.2 2.2 %collective-permute-start.11 = (bf16[128,1024]{1,0:T(8,128)(2,1)S(1)}, bf16[128,1024]{1,0:T(8,128)(2,1)S(1)}, u32[]{:S(2)}, u32[]{:S(2)}) collective-permute-start(bf16[128,1024]{1,0:T(8,128)(2,1)S(1)} %fusion.58), channel_id=1, source_target_pairs={{8,0},{0,8},{9,1},{1,9},{10,2},{2,10},{11,3},{3,11},{12,4},{4,12},... | collective-permute-start | bytes 786440 | tf_op jit(solution)/shard_map/ppermute | solution.py:381
  84.5 2.0 %pair_grads.2 = (bf16[8,128,128]{2,1,0:T(8,128)(2,1)S(1)}, bf16[8,128,128]{2,1,0:T(8,128)(2,1)S(1)}, bf16[8,128,128]{2,1,0:T(8,128)(2,1)S(1)}, bf16[8,128,128]{2,1,0:T(8,128)(2,1)S(1)}) custom-call(s32[5]{0:T(128)S(1)} %stack.52.where_ref, bf16[128,1024]{1,0:T(8,128)(2,1)S(1)} %collective-permute-done.6.rest_0_, ...), custom_call_target="tpu_custom_call" | custom-call | flops 268435456 | bytes 3145728 | tf_op jit(solution)/shard_map/pair_grads/pallas_call | solution.py:56
  86.6 5.0 %collective-permute-start.19 = (bf16[8,128,128]{2,1,0:T(8,128)(2,1)S(1)}, bf16[8,128,128]{2,1,0:T(8,128)(2,1)S(1)}, u32[]{:S(2)}, u32[]{:S(2)}) collective-permute-start(bf16[8,128,128]{2,1,0:T(8,128)(2,1)S(1)} %get-tuple-element.31), channel_id=1, source_target_pairs={{0,1},{1,0},{2,3},{3,2},{4,5},{5,4},{6,7},{7,6},{8,9},{9,8},{10,11... | collective-permute-start | bytes 786440 | tf_op jit(solution)/shard_map/ppermute | solution.py:351
  94.2 2.0 %pair_grads.3 = (bf16[8,128,128]{2,1,0:T(8,128)(2,1)S(1)}, bf16[8,128,128]{2,1,0:T(8,128)(2,1)S(1)}, bf16[8,128,128]{2,1,0:T(8,128)(2,1)S(1)}, bf16[8,128,128]{2,1,0:T(8,128)(2,1)S(1)}) custom-call(s32[5]{0:T(128)S(1)} %stack.52.where_ref, bf16[128,1024]{1,0:T(8,128)(2,1)S(1)} %collective-permute-done.7.rest_0_, ...), custom_call_target="tpu_custom_call" | custom-call | flops 268435456 | bytes 3145728 | tf_op jit(solution)/shard_map/pair_grads/pallas_call | solution.py:56
  97.8 2.2 %weight_half.2 = bf16[512,1024]{1,0:T(8,128)(2,1)S(1)} custom-call(s32[4]{0:T(128)S(1)} %pad_add_fusion.where_ref, bf16[1024,1024]{1,0:T(8,128)(2,1)S(1)} %flip.1.flipped_ref, bf16[128,1024]{1,0:T(8,128)(2,1)S(1)} %bitcast.184, bf16[128,1024]{1,0:T(8,128)(2,1)S(1)} %bitcast.187, bf16[128,1024]{1,0:T(8,128)(2,1)S(1)} %bitcast_select_fusion.10.rest_2_, ...), custom_call_target="tpu_custom_call" | custom-call | flops 1073741824 | bytes 6291456 | tf_op jit(solution)/shard_map/weight_half/pallas_call | solution.py:231
  102.2 3.5 %collective-permute-done.21.rest_3_ = bf16[8,128,128]{2,1,0:T(8,128)(2,1)S(1)} collective-permute-done((bf16[8,128,128]{2,1,0:T(8,128)(2,1)S(1)}, bf16[8,128,128]{2,1,0:T(8,128)(2,1)S(1)}, u32[]{:S(2)}, u32[]{:S(2)}) %collective-permute-start.21) | collective-permute-done | bytes 262176 | tf_op jit(solution)/shard_map/ppermute | solution.py:351
  105.8 4.8 %collective-permute-done.23.rest_6_ = bf16[8,128,128]{2,1,0:T(8,128)(2,1)S(1)} collective-permute-done((bf16[8,128,128]{2,1,0:T(8,128)(2,1)S(1)}, bf16[8,128,128]{2,1,0:T(8,128)(2,1)S(1)}, u32[]{:S(2)}, u32[]{:S(2)}) %collective-permute-start.23) | collective-permute-done | bytes 262176 | tf_op jit(solution)/shard_map/ppermute | solution.py:351
  110.6 5.9 %collective-permute-done.24.rest_7_ = bf16[8,128,128]{2,1,0:T(8,128)(2,1)S(1)} collective-permute-done((bf16[8,128,128]{2,1,0:T(8,128)(2,1)S(1)}, bf16[8,128,128]{2,1,0:T(8,128)(2,1)S(1)}, u32[]{:S(2)}, u32[]{:S(2)}) %collective-permute-start.24) | collective-permute-done | bytes 262176 | tf_op jit(solution)/shard_map/ppermute | solution.py:351
  124.3 3.0 %collective-permute-start.26 = (bf16[4,128,128]{2,1,0:T(8,128)(2,1)S(1)}, bf16[4,128,128]{2,1,0:T(8,128)(2,1)S(1)}, u32[]{:S(2)}, u32[]{:S(2)}) collective-permute-start(bf16[4,128,128]{2,1,0:T(8,128)(2,1)S(1)} %get-tuple-element.60), channel_id=1, source_target_pairs={{0,16},{8,24},{16,0},{24,8},{1,17},{9,25},{17,1},{25,9},{2,18},{10... | collective-permute-start | bytes 393224 | tf_op jit(solution)/shard_map/ppermute | solution.py:270
  128.4 2.2 %weight_half.3 = (f32[128,1024]{1,0:T(8,128)S(1)}, bf16[128,1024]{1,0:T(8,128)(2,1)S(1)}, bf16[128,1024]{1,0:T(8,128)(2,1)S(1)}, bf16[128,1024]{1,0:T(8,128)(2,1)S(1)}) custom-call(s32[4]{0:T(128)S(1)} %pad_add_fusion.1.where_ref, bf16[1024,1024]{1,0:T(8,128)(2,1)S(1)} %flip.1.flipped_ref, bf16[128,1024]{1,0:T(8,128)(2,1)S(1)} %bitcast.185, ...), custom_call_target="tpu_custom_call" | custom-call | flops 1073741824 | bytes 6291456 | tf_op jit(solution)/shard_map/weight_half/pallas_call | solution.py:231
  130.6 2.4 %collective-permute-start.13 = (bf16[128,1024]{1,0:T(8,128)(2,1)S(1)}, bf16[128,1024]{1,0:T(8,128)(2,1)S(1)}, u32[]{:S(2)}, u32[]{:S(2)}) collective-permute-start(bf16[128,1024]{1,0:T(8,128)(2,1)S(1)} %get-tuple-element.27), channel_id=1, source_target_pairs={{0,4},{2,6},{4,0},{6,2},{1,5},{3,7},{5,1},{7,3},{8,12},{10,14},{12... | collective-permute-start | bytes 786440 | tf_op jit(solution)/shard_map/ppermute | solution.py:437
  135.1 10.0 %collective-permute-done.13 = bf16[128,1024]{1,0:T(8,128)(2,1)S(1)} collective-permute-done((bf16[128,1024]{1,0:T(8,128)(2,1)S(1)}, bf16[128,1024]{1,0:T(8,128)(2,1)S(1)}, u32[]{:S(2)}, u32[]{:S(2)}) %collective-permute-start.13) | collective-permute-done | bytes 262176 | tf_op jit(solution)/shard_map/ppermute | solution.py:437
  145.1 14.8 %collective-permute-done.15 = bf16[128,1024]{1,0:T(8,128)(2,1)S(1)} collective-permute-done((bf16[128,1024]{1,0:T(8,128)(2,1)S(1)}, bf16[128,1024]{1,0:T(8,128)(2,1)S(1)}, u32[]{:S(2)}, u32[]{:S(2)}) %collective-permute-start.15) | collective-permute-done | bytes 262176 | tf_op jit(solution)/shard_map/ppermute | solution.py:437
  (119 shorter events, 59.5 us)
Async XLA Ops:
  2.4 15.5 %collective-permute-start.16 = (s32[8,256]{1,0:T(8,128)}, s32[8,256]{1,0:T(8,128)}, u32[]{:S(2)}, u32[]{:S(2)}) collective-permute-start(s32[8,256]{1,0:T(8,128)} %reshape.84), channel_id=1, source_target_pairs={{0,1},{1,0},{2,3},{3,2},{4,5},{5,4},{6,7},{7,6},{8,9},{9,8},{10,11... | collective-permute-start | bytes 24584 | tf_op jit(solution)/shard_map/ppermute | solution.py:351
  3.7 15.5 %collective-permute-start.17 = (s32[8,256]{1,0:T(8,128)}, s32[8,256]{1,0:T(8,128)}, u32[]{:S(2)}, u32[]{:S(2)}) collective-permute-start(s32[8,256]{1,0:T(8,128)} %reshape.85), channel_id=1, source_target_pairs={{0,2},{1,3},{2,0},{3,1},{4,6},{5,7},{6,4},{7,5},{8,10},{9,11},{10,... | collective-permute-start | bytes 24584 | tf_op jit(solution)/shard_map/ppermute | solution.py:351
  5.6 14.9 %collective-permute-start.18 = (s32[8,256]{1,0:T(8,128)}, s32[8,256]{1,0:T(8,128)}, u32[]{:S(2)}, u32[]{:S(2)}) collective-permute-start(s32[8,256]{1,0:T(8,128)} %reshape.86), channel_id=1, source_target_pairs={{0,3},{1,2},{2,1},{3,0},{4,7},{5,6},{6,5},{7,4},{8,11},{9,10},{10,... | collective-permute-start | bytes 24584 | tf_op jit(solution)/shard_map/ppermute | solution.py:351
  8.7 18.3 %collective-permute-start.1 = (bf16[128,1024]{1,0:T(8,128)(2,1)}, bf16[128,1024]{1,0:T(8,128)(2,1)}, u32[]{:S(2)}, u32[]{:S(2)}) collective-permute-start(bf16[128,1024]{1,0:T(8,128)(2,1)} %fusion.34), channel_id=1, source_target_pairs={{24,16},{25,17},{26,18},{27,19},{28,20},{29,21},{30,22},{31,23}} | collective-permute-start | bytes 786440 | tf_op jit(solution)/shard_map/ppermute | solution.py:381
  11.6 12.0 %collective-permute-start = (bf16[128,1024]{1,0:T(8,128)(2,1)}, bf16[128,1024]{1,0:T(8,128)(2,1)}, u32[]{:S(2)}, u32[]{:S(2)}) collective-permute-start(bf16[128,1024]{1,0:T(8,128)(2,1)} %fusion.28), channel_id=1, source_target_pairs={{24,16},{25,17},{26,18},{27,19},{28,20},{29,21},{30,22},{31,23}} | collective-permute-start | bytes 786440 | tf_op jit(solution)/shard_map/ppermute | solution.py:381
  25.6 19.0 %collective-permute-start.3 = (bf16[128,1024]{1,0:T(8,128)(2,1)S(1)}, bf16[128,1024]{1,0:T(8,128)(2,1)S(1)}, u32[]{:S(2)}, u32[]{:S(2)}) collective-permute-start(bf16[128,1024]{1,0:T(8,128)(2,1)S(1)} %fusion.31), channel_id=1, source_target_pairs={{16,8},{24,16},{17,9},{25,17},{18,10},{26,18},{19,11},{27,19},{20,... | collective-permute-start | bytes 786440 | tf_op jit(solution)/shard_map/ppermute | solution.py:381
  29.0 12.8 %collective-permute-start.2 = (bf16[128,1024]{1,0:T(8,128)(2,1)S(1)}, bf16[128,1024]{1,0:T(8,128)(2,1)S(1)}, u32[]{:S(2)}, u32[]{:S(2)}) collective-permute-start(bf16[128,1024]{1,0:T(8,128)(2,1)S(1)} %fusion.37), channel_id=1, source_target_pairs={{16,8},{24,16},{17,9},{25,17},{18,10},{26,18},{19,11},{27,19},{20,... | collective-permute-start | bytes 786440 | tf_op jit(solution)/shard_map/ppermute | solution.py:381
  42.7 9.5 %collective-permute-start.4 = (bf16[128,1024]{1,0:T(8,128)(2,1)S(1)}, bf16[128,1024]{1,0:T(8,128)(2,1)S(1)}, u32[]{:S(2)}, u32[]{:S(2)}) collective-permute-start(bf16[128,1024]{1,0:T(8,128)(2,1)S(1)} %fusion.43), channel_id=1, source_target_pairs={{8,0},{16,8},{24,16},{9,1},{17,9},{25,17},{10,2},{18,10},{26,18},{... | collective-permute-start | bytes 786440 | tf_op jit(solution)/shard_map/ppermute | solution.py:381
  45.6 12.3 %collective-permute-start.5 = (bf16[128,1024]{1,0:T(8,128)(2,1)S(1)}, bf16[128,1024]{1,0:T(8,128)(2,1)S(1)}, u32[]{:S(2)}, u32[]{:S(2)}) collective-permute-start(bf16[128,1024]{1,0:T(8,128)(2,1)S(1)} %fusion.40), channel_id=1, source_target_pairs={{8,0},{16,8},{24,16},{9,1},{17,9},{25,17},{10,2},{18,10},{26,18},{... | collective-permute-start | bytes 786440 | tf_op jit(solution)/shard_map/ppermute | solution.py:381
  53.2 10.3 %collective-permute-start.6 = (bf16[128,1024]{1,0:T(8,128)(2,1)S(1)}, bf16[128,1024]{1,0:T(8,128)(2,1)S(1)}, u32[]{:S(2)}, u32[]{:S(2)}) collective-permute-start(bf16[128,1024]{1,0:T(8,128)(2,1)S(1)} %fusion.49), channel_id=1, source_target_pairs={{8,0},{16,8},{24,16},{0,24},{9,1},{17,9},{25,17},{1,25},{10,2},{18... | collective-permute-start | bytes 786440 | tf_op jit(solution)/shard_map/ppermute | solution.py:381
  58.8 10.3 %collective-permute-start.7 = (bf16[128,1024]{1,0:T(8,128)(2,1)S(1)}, bf16[128,1024]{1,0:T(8,128)(2,1)S(1)}, u32[]{:S(2)}, u32[]{:S(2)}) collective-permute-start(bf16[128,1024]{1,0:T(8,128)(2,1)S(1)} %fusion.46), channel_id=1, source_target_pairs={{8,0},{16,8},{24,16},{0,24},{9,1},{17,9},{25,17},{1,25},{10,2},{18... | collective-permute-start | bytes 786440 | tf_op jit(solution)/shard_map/ppermute | solution.py:381
  70.0 10.3 %collective-permute-start.9 = (bf16[128,1024]{1,0:T(8,128)(2,1)S(1)}, bf16[128,1024]{1,0:T(8,128)(2,1)S(1)}, u32[]{:S(2)}, u32[]{:S(2)}) collective-permute-start(bf16[128,1024]{1,0:T(8,128)(2,1)S(1)} %fusion.52), channel_id=1, source_target_pairs={{8,0},{16,8},{0,16},{9,1},{17,9},{1,17},{10,2},{18,10},{2,18},{11,... | collective-permute-start | bytes 786440 | tf_op jit(solution)/shard_map/ppermute | solution.py:381
  81.2 12.1 %collective-permute-start.11 = (bf16[128,1024]{1,0:T(8,128)(2,1)S(1)}, bf16[128,1024]{1,0:T(8,128)(2,1)S(1)}, u32[]{:S(2)}, u32[]{:S(2)}) collective-permute-start(bf16[128,1024]{1,0:T(8,128)(2,1)S(1)} %fusion.58), channel_id=1, source_target_pairs={{8,0},{0,8},{9,1},{1,9},{10,2},{2,10},{11,3},{3,11},{12,4},{4,12},... | collective-permute-start | bytes 786440 | tf_op jit(solution)/shard_map/ppermute | solution.py:381
  86.6 13.3 %collective-permute-start.19 = (bf16[8,128,128]{2,1,0:T(8,128)(2,1)S(1)}, bf16[8,128,128]{2,1,0:T(8,128)(2,1)S(1)}, u32[]{:S(2)}, u32[]{:S(2)}) collective-permute-start(bf16[8,128,128]{2,1,0:T(8,128)(2,1)S(1)} %get-tuple-element.31), channel_id=1, source_target_pairs={{0,1},{1,0},{2,3},{3,2},{4,5},{5,4},{6,7},{7,6},{8,9},{9,8},{10,11... | collective-permute-start | bytes 786440 | tf_op jit(solution)/shard_map/ppermute | solution.py:351
  92.9 12.9 %collective-permute-start.21 = (bf16[8,128,128]{2,1,0:T(8,128)(2,1)S(1)}, bf16[8,128,128]{2,1,0:T(8,128)(2,1)S(1)}, u32[]{:S(2)}, u32[]{:S(2)}) collective-permute-start(bf16[8,128,128]{2,1,0:T(8,128)(2,1)S(1)} %get-tuple-element.33), channel_id=1, source_target_pairs={{0,3},{1,2},{2,1},{3,0},{4,7},{5,6},{6,5},{7,4},{8,11},{9,10},{10,... | collective-permute-start | bytes 786440 | tf_op jit(solution)/shard_map/ppermute | solution.py:351
  96.5 14.1 %collective-permute-start.23 = (bf16[8,128,128]{2,1,0:T(8,128)(2,1)S(1)}, bf16[8,128,128]{2,1,0:T(8,128)(2,1)S(1)}, u32[]{:S(2)}, u32[]{:S(2)}) collective-permute-start(bf16[8,128,128]{2,1,0:T(8,128)(2,1)S(1)} %get-tuple-element.36), channel_id=1, source_target_pairs={{0,2},{1,3},{2,0},{3,1},{4,6},{5,7},{6,4},{7,5},{8,10},{9,11},{10,... | collective-permute-start | bytes 786440 | tf_op jit(solution)/shard_map/ppermute | solution.py:351
  100.0 16.5 %collective-permute-start.24 = (bf16[8,128,128]{2,1,0:T(8,128)(2,1)S(1)}, bf16[8,128,128]{2,1,0:T(8,128)(2,1)S(1)}, u32[]{:S(2)}, u32[]{:S(2)}) collective-permute-start(bf16[8,128,128]{2,1,0:T(8,128)(2,1)S(1)} %get-tuple-element.37), channel_id=1, source_target_pairs={{0,3},{1,2},{2,1},{3,0},{4,7},{5,6},{6,5},{7,4},{8,11},{9,10},{10,... | collective-permute-start | bytes 786440 | tf_op jit(solution)/shard_map/ppermute | solution.py:351
  100.7 27.7 %collective-permute-start.12 = (bf16[512,1024]{1,0:T(8,128)(2,1)S(1)}, bf16[512,1024]{1,0:T(8,128)(2,1)S(1)}, u32[]{:S(2)}, u32[]{:S(2)}) collective-permute-start(bf16[512,1024]{1,0:T(8,128)(2,1)S(1)} %weight_half.2), channel_id=1, source_target_pairs={{0,1},{1,0},{2,3},{3,2},{4,5},{5,4},{6,7},{7,6},{8,9},{9,8},{10,11... | collective-permute-start | bytes 3145736 | tf_op jit(solution)/shard_map/ppermute | solution.py:429
  121.8 11.2 %collective-permute-start.25 = (bf16[4,128,128]{2,1,0:T(8,128)(2,1)S(1)}, bf16[4,128,128]{2,1,0:T(8,128)(2,1)S(1)}, u32[]{:S(2)}, u32[]{:S(2)}) collective-permute-start(bf16[4,128,128]{2,1,0:T(8,128)(2,1)S(1)} %get-tuple-element.58), channel_id=1, source_target_pairs={{0,8},{8,16},{16,24},{24,0},{1,9},{9,17},{17,25},{25,1},{2,10},{10... | collective-permute-start | bytes 393224 | tf_op jit(solution)/shard_map/ppermute | solution.py:270
  123.4 10.9 %collective-permute-start.27 = (bf16[4,128,128]{2,1,0:T(8,128)(2,1)S(1)}, bf16[4,128,128]{2,1,0:T(8,128)(2,1)S(1)}, u32[]{:S(2)}, u32[]{:S(2)}) collective-permute-start(bf16[4,128,128]{2,1,0:T(8,128)(2,1)S(1)} %get-tuple-element.59), channel_id=1, source_target_pairs={{0,24},{8,0},{16,8},{24,16},{1,25},{9,1},{17,9},{25,17},{2,26},{10... | collective-permute-start | bytes 393224 | tf_op jit(solution)/shard_map/ppermute | solution.py:270
  124.3 10.0 %collective-permute-start.26 = (bf16[4,128,128]{2,1,0:T(8,128)(2,1)S(1)}, bf16[4,128,128]{2,1,0:T(8,128)(2,1)S(1)}, u32[]{:S(2)}, u32[]{:S(2)}) collective-permute-start(bf16[4,128,128]{2,1,0:T(8,128)(2,1)S(1)} %get-tuple-element.60), channel_id=1, source_target_pairs={{0,16},{8,24},{16,0},{24,8},{1,17},{9,25},{17,1},{25,9},{2,18},{10... | collective-permute-start | bytes 393224 | tf_op jit(solution)/shard_map/ppermute | solution.py:270
  130.6 14.5 %collective-permute-start.13 = (bf16[128,1024]{1,0:T(8,128)(2,1)S(1)}, bf16[128,1024]{1,0:T(8,128)(2,1)S(1)}, u32[]{:S(2)}, u32[]{:S(2)}) collective-permute-start(bf16[128,1024]{1,0:T(8,128)(2,1)S(1)} %get-tuple-element.27), channel_id=1, source_target_pairs={{0,4},{2,6},{4,0},{6,2},{1,5},{3,7},{5,1},{7,3},{8,12},{10,14},{12... | collective-permute-start | bytes 786440 | tf_op jit(solution)/shard_map/ppermute | solution.py:437
  133.0 12.1 %collective-permute-start.14 = (bf16[128,1024]{1,0:T(8,128)(2,1)S(1)}, bf16[128,1024]{1,0:T(8,128)(2,1)S(1)}, u32[]{:S(2)}, u32[]{:S(2)}) collective-permute-start(bf16[128,1024]{1,0:T(8,128)(2,1)S(1)} %get-tuple-element.28), channel_id=1, source_target_pairs={{0,2},{2,0},{4,6},{6,4},{1,3},{3,1},{5,7},{7,5},{8,10},{10,8},{12,... | collective-permute-start | bytes 786440 | tf_op jit(solution)/shard_map/ppermute | solution.py:437
  134.3 25.6 %collective-permute-start.15 = (bf16[128,1024]{1,0:T(8,128)(2,1)S(1)}, bf16[128,1024]{1,0:T(8,128)(2,1)S(1)}, u32[]{:S(2)}, u32[]{:S(2)}) collective-permute-start(bf16[128,1024]{1,0:T(8,128)(2,1)S(1)} %get-tuple-element.29), channel_id=1, source_target_pairs={{0,6},{2,4},{4,2},{6,0},{1,7},{3,5},{5,3},{7,1},{8,14},{10,12},{12... | collective-permute-start | bytes 786440 | tf_op jit(solution)/shard_map/ppermute | solution.py:437
  (15 other events, 106.6 us)
